TPU v7x, 32 devices: a whole 2x2x4 slice. The times are simulated.
32 devices in a mesh: dp: 32 (over z, y, x, core).
Axes of the slice: x: 2, y: 2, z: 4, core: 2. Of those that a mesh axis runs over, the one named last changes fastest.
Arguments:
- tokens: bfloat16 [4096, 2048], P('dp'), may hold values from -6 to 6
- seq_lengths: int32 [32, 2, 4], P('dp'), may hold values from 0 to 64, as said below
- attn_gain: bfloat16 [2048], P('dp'), may hold values from 0.5 to 1.5
- attn_shift: bfloat16 [2048], P('dp'), may hold values from -1 to 1
- query_weight: bfloat16 [2048, 2048], P('dp'), may hold values from -0.125 to 0.125
- key_weight: bfloat16 [2048, 2048], P('dp'), may hold values from -0.125 to 0.125
- value_weight: bfloat16 [2048, 4096], P('dp'), may hold values from -0.125 to 0.125
- gate_weight: bfloat16 [2048, 4096], P('dp'), may hold values from -0.125 to 0.125
- out_weight: bfloat16 [4096, 2048], P('dp'), may hold values from -0.09375 to 0.09375
- mlp_gain: bfloat16 [2048], P('dp'), may hold values from 0.5 to 1.5
- mlp_shift: bfloat16 [2048], P('dp'), may hold values from -1 to 1
- mlp_gate: bfloat16 [2048, 4096], P('dp'), may hold values from -0.125 to 0.125
- mlp_up: bfloat16 [2048, 4096], P('dp'), may hold values from -0.125 to 0.125
- mlp_down: bfloat16 [4096, 2048], P('dp'), may hold values from -0.09375 to 0.09375
- cotangent: bfloat16 [4096, 2048], P('dp'), may hold values from -6 to 6
Outputs:
- output: bfloat16 [4096, 2048], P('dp')
- tokens_grad: float32 [4096, 2048], P('dp')
- attn_gain_grad: float32 [2048], P('dp')
- attn_shift_grad: float32 [2048], P('dp')
- query_weight_grad: float32 [2048, 2048], P('dp')
- key_weight_grad: float32 [2048, 2048], P('dp')
- value_weight_grad: float32 [2048, 4096], P('dp')
- gate_weight_grad: float32 [2048, 4096], P('dp')
- out_weight_grad: float32 [4096, 2048], P('dp')
- mlp_gain_grad: float32 [2048], P('dp')
- mlp_shift_grad: float32 [2048], P('dp')
- mlp_gate_grad: float32 [2048, 4096], P('dp')
- mlp_up_grad: float32 [2048, 4096], P('dp')
- mlp_down_grad: float32 [4096, 2048], P('dp')
Inputs may be any that keep to these rules, and one draw needn't show every extreme that they name: seq_lengths[d, m, :] lists the lengths of the sequences placed in micro-batch m of device d, packed from its first row in this order; 0 marks an unused slot; the lengths of one micro-batch add up to between 32 and 64; in every draw some micro-batch holds a single sequence of 64 tokens.
All inputs are finite; a program needn't handle non-finite values.
Results may differ from a plain program's by a relative error of at most 0.015.
Values may be sent and summed in bfloat16 or wider, within the bound.
A program may use at most 512 MiB of HBM per device.

v0:
```python
import functools

import jax
import jax.numpy as jnp
from jax import lax
from jax.experimental import pallas as pl
from jax.experimental.pallas import tpu as pltpu
from jax.sharding import PartitionSpec as P


HEADS = 8
NORM_EPS = 1e-05
GROUP_EPS = 1.0
BF = jnp.bfloat16
F32 = jnp.float32
MESH = pl.DeviceIdType.MESH
LANES = 128


CORE, NEAR = 1, 2
TILE = 16


class Layout:
    def __init__(self, count, shard):
        self.count, self.shard = count, shard
        self.far_bit = 3 if (4 * shard) % LANES == 0 and count >= 32 else 2
        self.far = 1 << self.far_bit
        self.bits = count.bit_length() - 1
        self.rep_bits = [b for b in range(2, self.bits) if b != self.far_bit]
        self.reps = count // 8
        self.team = (CORE, NEAR, self.far, CORE | NEAR, CORE | self.far, NEAR | self.far,
                     CORE | NEAR | self.far)
        self.masks = self.team + tuple(
            1 << b for b in range(self.bits) if (1 << b) not in self.team
        )

    def place(self, device):
        return ((device // self.far) % 2) * 4 + device % 4

    def rep(self, device):
        total = 0
        for i, b in enumerate(self.rep_bits):
            total = total + ((device // (1 << b)) % 2) * (1 << i)
        return total

    def device(self, rep, place):
        total = place % 4 + (place // 4) * self.far
        for i, b in enumerate(self.rep_bits):
            total += ((rep >> i) & 1) << b
        return total

    def low(self, rel):
        return (rel & -rel).bit_length() - 1 if rel else len(self.rep_bits)

    def mask(self, rel):
        return 1 << self.rep_bits[self.low(rel)]

    def sources(self, rel):
        return [rel | (1 << i) for i in range(self.low(rel))]

    def pieces(self, width):
        if self.far_bit == 2:
            return [(0, width)]
        size = 4 * self.shard
        order = []
        for hi in range(self.count // 16):
            for b2 in range(2):
                for b3 in range(2):
                    order.append(((hi * 4 + b3 * 2 + b2) * size, size))
        return order


def flip_device(device, mask):
    other, bit = device, 0
    while mask >> bit:
        if (mask >> bit) & 1:
            other = other + (1 - 2 * ((device // (1 << bit)) % 2)) * (1 << bit)
        bit += 1
    return other


def xor_index(static, own, size):
    total, bit = 0, 1
    while bit < size:
        own_bit = (own // bit) % 2
        total = total + bit * (1 - own_bit if static & bit else own_bit)
        bit *= 2
    return total


def layer_norm(values, gain_vec, shift_vec):
    center = values - jnp.mean(values, axis=-1, keepdims=True)
    spread = jnp.mean(center * center, axis=-1, keepdims=True)
    return center * lax.rsqrt(spread + NORM_EPS) * gain_vec + shift_vec


def layer_norm_back(values, gain_vec, grads):
    center = values - jnp.mean(values, axis=-1, keepdims=True)
    scale = lax.rsqrt(jnp.mean(center * center, axis=-1, keepdims=True) + NORM_EPS)
    z = center * scale
    e = grads * gain_vec
    part = scale * (
        e - jnp.mean(e, axis=-1, keepdims=True) - z * jnp.mean(e * z, axis=-1, keepdims=True)
    )
    gain_part = jnp.sum(grads * z, axis=0, keepdims=True)
    shift_part = jnp.sum(grads, axis=0, keepdims=True)
    return part, gain_part, shift_part


def to_weight_order(values, pieces):
    return jnp.concatenate([values[:, at : at + size] for at, size in pieces], axis=1)


def from_weight_order(values, pieces):
    size = pieces[0][1]
    where = {at: i * size for i, (at, _) in enumerate(pieces)}
    return jnp.concatenate([values[:, where[at] : where[at] + size] for at in sorted(where)], axis=1)


class Links:
    def __init__(self, layout, send_sems, recv_sems, local_sems):
        self.layout = layout
        self.device = lax.axis_index("dp")
        self.send_sems, self.recv_sems, self.local_sems = send_sems, recv_sems, local_sems
        self.made, self.locals, self.sent = [], [], []

    def greet(self, masks):
        barrier = pltpu.get_barrier_semaphore()
        for mask in masks:
            pl.semaphore_signal(
                barrier, inc=1, device_id=(flip_device(self.device, mask),), device_id_type=MESH
            )
        pl.semaphore_wait(barrier, len(masks))

    def send(self, source, target, mask):
        index = len(self.made)
        copy = pltpu.make_async_remote_copy(
            src_ref=source,
            dst_ref=target,
            send_sem=self.send_sems.at[index],
            recv_sem=self.recv_sems.at[index],
            device_id=(flip_device(self.device, mask),),
            device_id_type=MESH,
        )
        copy.start()
        self.made.append(copy)
        return copy

    def local(self, source, target):
        copy = pltpu.make_async_copy(source, target, self.local_sems.at[len(self.locals)])
        copy.start()
        self.locals.append(copy)
        return copy

    def swap_done(self, copy):
        copy.wait()
        self.sent.append(copy)

    def finish(self):
        for copy in self.made:
            if not any(copy is other for other in self.sent):
                copy.wait_send()


def gather_steps(links, own, out):
    got = {}
    far = links.layout.far

    def begin():
        got["an"] = links.send(own.at[0], out.at[2], NEAR)
        got["bf"] = links.send(own.at[1], out.at[5], far)
        got["bn"] = links.send(own.at[1], out.at[3], NEAR)
        got["af"] = links.send(own.at[0], out.at[4], far)
        got["c"] = [links.send(own.at[i], out.at[8 + i], CORE) for i in range(2)]

    def relay():
        got["an"].wait_recv()
        got["anf"] = links.send(out.at[2], out.at[6], far)
        got["c"].append(links.send(out.at[2], out.at[10], CORE))
        got["bf"].wait_recv()
        got["bnf"] = links.send(out.at[5], out.at[7], NEAR)
        got["c"].append(links.send(out.at[5], out.at[13], CORE))
        got["bn"].wait_recv()
        got["c"].append(links.send(out.at[3], out.at[11], CORE))
        got["af"].wait_recv()
        got["c"].append(links.send(out.at[4], out.at[12], CORE))

    def end():
        got["anf"].wait_recv()
        got["c"].append(links.send(out.at[6], out.at[14], CORE))
        got["bnf"].wait_recv()
        got["c"].append(links.send(out.at[7], out.at[15], CORE))
        for copy in got["c"]:
            copy.wait_recv()

    return [begin, relay, end]


def gather_steps_light(links, own, out):
    got = {}
    far = links.layout.far

    def begin():
        got["af"] = links.send(own.at[0], out.at[4], far)
        got["bf"] = links.send(own.at[1], out.at[5], far)
        got["an"] = links.send(own.at[0], out.at[2], NEAR)
        got["bn"] = links.send(own.at[1], out.at[3], NEAR)
        got["c"] = [links.send(own.at[i], out.at[8 + i], CORE) for i in range(2)]

    def relay():
        for i, name in enumerate(("af", "bf")):
            got[name].wait_recv()
            got[name + "n"] = links.send(out.at[4 + i], out.at[6 + i], NEAR)
            got["c"].append(links.send(out.at[4 + i], out.at[12 + i], CORE))
        for i, name in enumerate(("an", "bn")):
            got[name].wait_recv()
            got["c"].append(links.send(out.at[2 + i], out.at[10 + i], CORE))

    def end():
        for i, name in enumerate(("afn", "bfn")):
            got[name].wait_recv()
            got["c"].append(links.send(out.at[6 + i], out.at[14 + i], CORE))
        for copy in got["c"]:
            copy.wait_recv()

    return [begin, relay, end]


GATHER_COPIES = 14


def scatter_steps(links, parts, even, cores, taken, finish):
    got = {}
    far = links.layout.far

    def total(block):
        return even[block].astype(F32) + cores[block].astype(F32)

    def begin():
        got["load"] = links.local(parts.at[pl.ds(0, 8)], even)
        got["last"] = links.send(parts.at[pl.ds(14, 2)], cores.at[pl.ds(6, 2)], CORE)
        got["mid"] = links.send(parts.at[pl.ds(10, 4)], cores.at[pl.ds(2, 4)], CORE)
        got["own"] = links.send(parts.at[pl.ds(8, 2)], cores.at[pl.ds(0, 2)], CORE)

    def corners():
        got["load"].wait()
        got["last"].wait_recv()
        even[6] = total(6).astype(BF)
        got["anf"] = links.send(even.at[6], taken.at[0], far)
        even[7] = total(7).astype(BF)
        got["bnf"] = links.send(even.at[7], taken.at[1], NEAR)
        got["mid"].wait_recv()
        even[4] = total(4).astype(BF)
        got["af"] = links.send(even.at[4], taken.at[2], far)
        even[3] = total(3).astype(BF)
        got["bn"] = links.send(even.at[3], taken.at[3], NEAR)

    def relay():
        got["anf"].wait_recv()
        even[2] = (total(2) + taken[0].astype(F32)).astype(BF)
        got["an"] = links.send(even.at[2], taken.at[4], NEAR)
        got["bnf"].wait_recv()
        even[5] = (total(5) + taken[1].astype(F32)).astype(BF)
        got["bf"] = links.send(even.at[5], taken.at[5], far)

    def end():
        got["own"].wait_recv()
        for name in ("af", "an"):
            got[name].wait_recv()
        finish(0, total(0) + taken[2].astype(F32) + taken[4].astype(F32))
        for name in ("bn", "bf"):
            got[name].wait_recv()
        finish(1, total(1) + taken[3].astype(F32) + taken[5].astype(F32))

    return [begin, corners, relay, end]


def scatter_steps_light(links, parts, even, cores, taken, finish):
    got = {}
    far = links.layout.far

    def total(block):
        return even[block].astype(F32) + cores[block].astype(F32)

    def begin():
        got["load"] = links.local(parts.at[pl.ds(0, 8)], even)
        got["last"] = links.send(parts.at[pl.ds(14, 2)], cores.at[pl.ds(6, 2)], CORE)
        got["mid"] = links.send(parts.at[pl.ds(10, 4)], cores.at[pl.ds(2, 4)], CORE)
        got["own"] = links.send(parts.at[pl.ds(8, 2)], cores.at[pl.ds(0, 2)], CORE)

    def corners():
        got["load"].wait()
        got["last"].wait_recv()
        for i in range(2):
            even[6 + i] = total(6 + i).astype(BF)
            got["nf", i] = links.send(even.at[6 + i], taken.at[i], NEAR)
        got["mid"].wait_recv()
        for i in range(2):
            even[2 + i] = total(2 + i).astype(BF)
            got["n", i] = links.send(even.at[2 + i], taken.at[2 + i], NEAR)

    def relay():
        for i in range(2):
            got["nf", i].wait_recv()
            even[4 + i] = (total(4 + i) + taken[i].astype(F32)).astype(BF)
            got["f", i] = links.send(even.at[4 + i], taken.at[4 + i], far)

    def end():
        got["own"].wait_recv()
        for i in range(2):
            got["n", i].wait_recv()
            got["f", i].wait_recv()
            finish(i, total(i) + taken[2 + i].astype(F32) + taken[4 + i].astype(F32))

    return [begin, corners, relay, end]


SCATTER_COPIES = 9


def scatter_scratch(half, width):
    return [
        pltpu.VMEM((8, half, width), BF),
        pltpu.VMEM((8, half, width), BF),
        pltpu.VMEM((6, half, width), BF),
    ]


def gather_stream(links, items, lag):
    layout = links.layout
    made = [{} for _ in items]

    def spread(i, rel, source):
        slot = items[i][2]
        for bit in range(layout.low(rel)):
            goal = rel | (1 << bit)
            made[i][goal] = links.send(source, slot(rel), layout.mask(1 << bit))

    def step(k):
        def run():
            if k < len(items):
                ready, own, _ = items[k]
                ready()
                spread(k, 0, own)
            if k >= lag:
                i = k - lag
                for rel in range(2, layout.reps, 2):
                    made[i][rel].wait_recv()
                    spread(i, rel, items[i][2](rel))

        return run

    def end():
        for copies in made:
            for rel in range(1, layout.reps, 2):
                copies[rel].wait_recv()

    return [step(k) for k in range(len(items) + lag)], end


def scatter_stream(links, items, window, lag):
    layout = links.layout
    made = [{} for _ in items]
    loads = [None for _ in items]
    stay = range(0, layout.reps, 2)

    def begin(i):
        part, keep, taken, _, paired = items[i]
        loads[i] = [links.local(part(rel), keep(rel // 2)) for rel in stay]
        for rel in range(layout.reps - 1, 0, -2):
            if not paired:
                made[i][rel] = links.send(part(rel), taken(rel - 1), layout.mask(rel))

    def total(i, rel):
        _, keep, taken, _, paired = items[i]
        sources = [source for source in layout.sources(rel) if not (paired and source & 1)]
        for source in sources:
            made[i][source].wait_recv()
        value = keep(rel // 2)[...].astype(F32)
        for source in sources:
            value = value + taken(source - 1)[...].astype(F32)
        return value

    def pass_on(i):
        _, keep, taken, _, paired = items[i]
        for load in loads[i]:
            load.wait()
        for rel in stay[:0:-1]:
            if not (paired and layout.low(rel) == 1):
                keep(rel // 2)[...] = total(i, rel).astype(BF)
            made[i][rel] = links.send(keep(rel // 2), taken(rel - 1), layout.mask(rel))

    def step(k):
        def run():
            if k < len(items):
                begin(k)
            if window <= k < len(items) + window:
                pass_on(k - window)
            if k >= window + lag:
                items[k - window - lag][3](total(k - window - lag, 0))

        return run

    return [step(k) for k in range(len(items) + window + lag)]


def pair_stream(links, items, window):
    layout = links.layout
    made = [{} for _ in items]

    def begin(i):
        part, keep, taken, _ = items[i]
        for k in range(layout.reps // 2):
            made[i][k] = (
                links.local(part(2 * k), keep(k)),
                links.send(part(2 * k + 1), taken(k), layout.mask(1)),
            )

    def end(i):
        _, keep, taken, finish = items[i]
        for k, (load, copy) in made[i].items():
            load.wait()
            copy.wait_recv()
            finish(k, keep(k)[...].astype(F32) + taken(k)[...].astype(F32))

    def step(k):
        def run():
            if k < len(items):
                begin(k)
            if k >= window:
                end(k - window)

        return run

    return [step(k) for k in range(len(items) + window)]


def interleave(stream, acts, first=1):
    acts = list(acts)
    for k, step in enumerate(stream):
        step()
        if k >= first and acts:
            acts.pop(0)()
    for act in acts:
        act()


def semaphores(copies, local_copies):
    return [
        pltpu.SemaphoreType.DMA((copies,)),
        pltpu.SemaphoreType.DMA((copies,)),
        pltpu.SemaphoreType.DMA((local_copies,)),
    ]


VMEM = pl.BlockSpec(memory_space=pltpu.VMEM)
HBM = pl.BlockSpec(memory_space=pl.ANY)


def kernel_params(call_id):
    return pltpu.CompilerParams(collective_id=call_id, has_side_effects=True)


def opening_kernel(
    layout, small, tokens, cot, query_w, key_w, value_w, gate_w, gate_src, up_src, out_src,
    small_all, x_all, cot_all, attn_w, gate_in, up_in, out_w,
    small_buf, gain_buf, normed_buf, attn_own, out_own, gate_own, up_own, send_sems, recv_sems, local_sems,
):
    links = Links(layout, send_sems, recv_sems, local_sems)
    device = links.device
    place, rep = layout.place(device), layout.rep(device)
    _, half, width = tokens.shape
    shard = layout.shard

    def place_at(mask):
        return layout.place(flip_device(device, mask)) if mask else place

    edges, columns = 0, []
    for weight in (query_w, key_w, value_w, gate_w):
        size = weight.shape[1] // HEADS
        columns.append((weight, size, edges))
        edges += size

    def column(weight, size, where):
        return weight.at[:, pl.ds(pl.multiple_of(where * size, LANES), size)]

    mine = links.local(small, small_buf.at[pl.ds(device, 1)])
    own_loads = [
        links.local(column(weight, size, place), attn_own.at[:, pl.ds(at, size)])
        for weight, size, at in columns
    ]
    out_load = links.local(out_src, out_own)
    gate_load = links.local(gate_src.at[place], gate_own)
    up_load = links.local(up_src.at[place], up_own)
    links.greet(layout.masks)
    mine.wait()

    def small_step(b):
        size = 1 << b
        part = small_buf.at[pl.ds((device // size) * size, size)]
        return links.send(part, part, size)

    attn_in, later_in = {}, []

    def attn_exchange(mask):
        attn_in[mask] = [
            links.send(
                column(weight, size, place_at(mask)),
                attn_w.at[rep, place, :, pl.ds(at, size)],
                mask,
            )
            for weight, size, at in columns
        ]

    def hidden_exchange(mask):
        for source, target in ((gate_src, gate_in), (up_src, up_in)):
            later_in.append(links.send(source.at[place_at(mask)], target.at[place], mask))

    small_copy = small_step(0)
    for mask in layout.team[:3]:
        attn_exchange(mask)
    for load in own_loads:
        load.wait()
    keeps = [links.local(attn_own, attn_w.at[rep, place])]

    def attn_item(mask):
        at = place_at(mask)

        def ready():
            for copy in attn_in.get(mask, ()):
                copy.wait_recv()

        own = attn_w.at[rep, at] if mask else attn_own
        return ready, own, lambda rel: attn_w.at[xor_index(rel, rep, layout.reps), at]

    def row_item(own, target, part):
        return (
            lambda: None,
            own.at[part],
            lambda rel: target.at[xor_index(rel, rep, layout.reps), part],
        )

    items = [attn_item(0)] + [row_item(out_own, out_w, part) for part in range(4)]
    items += [attn_item(mask) for mask in layout.team]
    out_load.wait()
    keeps.append(links.local(out_own, out_w.at[rep]))
    steps, stream_end = gather_stream(links, items, 3)
    steps[0]()
    for b in range(1, layout.bits):
        small_copy.wait_recv()
        small_copy = small_step(b)
        if b < 5:
            attn_exchange(layout.team[2 + b])
        if b == 2:
            steps[1]()
    steps[2]()
    small_copy.wait_recv()
    keeps.append(links.local(small_buf, small_all))

    per = LANES // shard
    for k in range(width // LANES):
        rows = small_buf[k * per].astype(F32)
        for i in range(1, per):
            rows = rows + small_buf[k * per + i].astype(F32)
        gain_buf[:, k * LANES : (k + 1) * LANES] = rows
    gain, shift = gain_buf[0:1, :], gain_buf[1:2, :]
    pieces = layout.pieces(width)

    def norm_rows(i, carry):
        part = i // (half // TILE)
        at = pl.ds(pl.multiple_of((i % (half // TILE)) * TILE, TILE), TILE)
        normed = layer_norm(tokens[part, at, :].astype(F32), gain, shift)
        normed_buf[part, at, :] = to_weight_order(normed, pieces).astype(BF)
        return carry

    lax.fori_loop(0, 2 * half // TILE, norm_rows, 0)
    keeps.append(links.local(normed_buf, x_all.at[pl.ds(0, 2)]))
    keeps.append(links.local(cot, cot_all.at[pl.ds(0, 2)]))
    for own, target, load in ((gate_own, gate_in, gate_load), (up_own, up_in, up_load)):
        load.wait()
        keeps.append(links.local(own, target.at[place]))

    def exchange_some(masks):
        return lambda: [hidden_exchange(mask) for mask in masks]

    x_steps = gather_steps_light(links, normed_buf, x_all)
    cot_steps = gather_steps_light(links, cot, cot_all)
    acts = x_steps[:1] + [lambda: None] + x_steps[1:2] + [lambda: None] + x_steps[2:]
    acts += [exchange_some(layout.team[:2]), exchange_some(layout.team[2:4])]
    acts += cot_steps[:1] + [exchange_some(layout.team[4:6])] + cot_steps[1:2]
    acts += [exchange_some(layout.team[6:])] + cot_steps[2:]
    interleave(steps[3:], acts, 0)
    stream_end()
    for copy in later_in:
        copy.wait_recv()
    for copy in keeps:
        copy.wait()
    links.finish()


def opening_call(layout, small, tokens, cot, attn_weights, gate_src, up_src, out_src):
    reps, shard = layout.reps, layout.shard
    rows, width = tokens.shape
    half = rows // 2
    attn_cols = sum(w.shape[1] for w in attn_weights) // HEADS
    ff_cols = gate_src.shape[2]
    out_shape = (4, out_src.shape[0] // 4, out_src.shape[1])
    copies = 7 * 4 + 7 * 2 + 12 * (reps - 1) + 2 * GATHER_COPIES + layout.bits
    return pl.pallas_call(
        functools.partial(opening_kernel, layout),
        out_shape=(
            jax.ShapeDtypeStruct((layout.count, 8, LANES), BF),
            jax.ShapeDtypeStruct((16, half, width), BF),
            jax.ShapeDtypeStruct((16, half, width), BF),
            jax.ShapeDtypeStruct((reps, 8, shard, attn_cols), BF),
            jax.ShapeDtypeStruct((8, shard, ff_cols), BF),
            jax.ShapeDtypeStruct((8, shard, ff_cols), BF),
            jax.ShapeDtypeStruct((reps,) + out_shape, BF),
        ),
        in_specs=[HBM, VMEM] + [HBM] * 8,
        out_specs=(HBM,) * 7,
        scratch_shapes=[
            pltpu.VMEM((layout.count, 8, LANES), BF),
            pltpu.VMEM((8, width), F32),
            pltpu.VMEM((2, half, width), BF),
            pltpu.VMEM((shard, attn_cols), BF),
            pltpu.VMEM(out_shape, BF),
            pltpu.VMEM((shard, ff_cols), BF),
            pltpu.VMEM((shard, ff_cols), BF),
        ]
        + semaphores(copies, 18),
        compiler_params=kernel_params(0),
        name="opening",
    )(
        small, tokens.reshape(2, half, width), cot.reshape(2, half, width), *attn_weights,
        gate_src, up_src, out_src.reshape(out_shape),
    )


def turn_kernel(
    layout, parts, tokens, gains, gate_in, up_in, down_in,
    hidden, all_rows, gate_w, up_w, down_w,
    even, cores, taken, normed_buf, send_sems, recv_sems, local_sems,
):
    links = Links(layout, send_sems, recv_sems, local_sems)
    rep = layout.rep(links.device)
    _, half, width = tokens.shape
    links.greet((CORE, NEAR, layout.far) + tuple(1 << b for b in layout.rep_bits))
    keeps = [links.local(gate_in, gate_w.at[rep]), links.local(up_in, up_w.at[rep])]
    downs = []
    for i in range(layout.reps // 2):
        slot = down_w.at[xor_index(2 * i, rep, layout.reps)]
        keeps.append(links.local(down_in.at[i], slot))
        downs.append(links.send(down_in.at[i], slot, layout.mask(1)))

    def item(own, target, part):
        at = pl.ds(part * 2, 2)
        return (
            lambda: None,
            own.at[at],
            lambda rel: target.at[xor_index(rel, rep, layout.reps), at],
        )

    items = [item(gate_in, gate_w, part) for part in range(4)]
    items += [item(up_in, up_w, part) for part in range(4)]
    steps, stream_end = gather_stream(links, items, 2)
    pieces = layout.pieces(width)

    def finish(part, value):
        hidden[part] = value + tokens[part].astype(F32)

        def norm_rows(i, carry):
            at = pl.ds(pl.multiple_of(i * TILE, TILE), TILE)
            normed = layer_norm(hidden[part, at, :], gains[0:1, :], gains[1:2, :])
            normed_buf[part, at, :] = to_weight_order(normed, pieces).astype(BF)
            return carry

        lax.fori_loop(0, half // TILE, norm_rows, 0)

    acts = scatter_steps_light(links, parts, even, cores, taken, finish)
    acts.append(lambda: keeps.append(links.local(normed_buf, all_rows.at[pl.ds(0, 2)])))
    acts += gather_steps_light(links, normed_buf, all_rows)
    acts.pop(0)()
    interleave(steps, acts, 0)
    stream_end()
    for copy in downs:
        copy.wait_recv()
    for copy in keeps:
        copy.wait()
    links.finish()


def turn_call(layout, parts, tokens, gains, gate_in, up_in, down_in):
    rows, width = tokens.shape
    half = rows // 2
    block = gate_in.shape
    return pl.pallas_call(
        functools.partial(turn_kernel, layout),
        out_shape=(
            jax.ShapeDtypeStruct((2, half, width), F32),
            jax.ShapeDtypeStruct((16, half, width), BF),
            jax.ShapeDtypeStruct((layout.reps,) + block, BF),
            jax.ShapeDtypeStruct((layout.reps,) + block, BF),
            jax.ShapeDtypeStruct((layout.reps,) + down_in.shape[1:], BF),
        ),
        in_specs=[HBM, VMEM, VMEM, VMEM, VMEM, VMEM],
        out_specs=(VMEM, HBM, HBM, HBM, HBM),
        scratch_shapes=scatter_scratch(half, width)
        + [pltpu.VMEM((2, half, width), BF)]
        + semaphores(
            8 * (layout.reps - 1) + layout.reps // 2 + SCATTER_COPIES + GATHER_COPIES,
            5 + layout.reps // 2,
        ),
        compiler_params=kernel_params(1),
        name="turn",
    )(parts.reshape(16, half, width), tokens.reshape(2, half, width), gains, gate_in, up_in, down_in)


def turn_back_kernel(
    layout, parts, hidden, out_grad, gains, down_p, gate_p,
    hidden_grad, all_rows, vectors, down_first, down_rest, gate_first, gate_rest,
    even, cores, taken, low_buf, sum_buf, down_l, down_y, gate_l, gate_y,
    send_sems, recv_sems, local_sems,
):
    links = Links(layout, send_sems, recv_sems, local_sems)
    rep = layout.rep(links.device)
    _, half, width = hidden.shape
    links.greet((CORE, NEAR, layout.far) + tuple(1 << b for b in layout.rep_bits))

    def item(part, keep, taken, at, first, rest):
        def finish(k, value):
            if k:
                rest[k - 1, at] = value.astype(rest.dtype)
            else:
                first[at] = value.astype(first.dtype)

        return (
            lambda rel: part.at[xor_index(rel, rep, layout.reps), at],
            lambda k: keep.at[k, at],
            lambda k: taken.at[k, at],
            finish,
        )

    pairs = [pl.ds(2 * part, 2) for part in range(4)]
    items = [item(down_p, down_l, down_y, at, down_first, down_rest) for at in range(4)]
    items += [item(gate_p, gate_l, gate_y, at, gate_first, gate_rest) for at in pairs]
    steps = pair_stream(links, items, 3)
    pieces = layout.pieces(width)
    vectors[...] = jnp.zeros_like(vectors)

    def finish(part, value):
        sum_buf[...] = value

        def rows(i, carry):
            at = pl.ds(pl.multiple_of(i * TILE, TILE), TILE)
            grads = from_weight_order(sum_buf[at, :], pieces)
            back, gain_part, shift_part = layer_norm_back(
                hidden[part, at, :], gains[0:1, :], grads
            )
            total = out_grad[part, at, :].astype(F32) + back
            hidden_grad[part, at, :] = total
            low_buf[part, at, :] = total.astype(BF)
            vectors[0:1, :] += gain_part
            vectors[1:2, :] += shift_part
            return carry

        lax.fori_loop(0, half // TILE, rows, 0)

    keeps = []
    acts = scatter_steps(links, parts, even, cores, taken, finish)
    acts.append(lambda: keeps.append(links.local(low_buf, all_rows.at[pl.ds(0, 2)])))
    acts += gather_steps(links, low_buf, all_rows)
    acts.pop(0)()
    interleave(steps, acts, 0)
    for copy in keeps:
        copy.wait()
    links.finish()


def replica_items(layout, rep, part, keep, taken, places, sums, paired=False):
    def item(at):
        def finish(value):
            sums[at] = value.astype(sums.dtype)

        return (
            lambda rel: part.at[rel // 2 if paired else xor_index(rel, rep, layout.reps), at],
            lambda i: keep.at[i, at],
            lambda i: taken.at[i, at],
            finish,
            paired,
        )

    return [item(at) for at in places]


def turn_back_call(layout, parts, hidden, out_grad, gains, down_p, gate_p):
    half, width = hidden.shape[1:]
    reps = layout.reps
    down_block, gate_block = down_p.shape[1:], gate_p.shape[1:]
    return pl.pallas_call(
        functools.partial(turn_back_kernel, layout),
        out_shape=(
            jax.ShapeDtypeStruct((2, half, width), F32),
            jax.ShapeDtypeStruct((16, half, width), BF),
            jax.ShapeDtypeStruct((8, width), F32),
            jax.ShapeDtypeStruct(down_block, F32),
            jax.ShapeDtypeStruct((reps // 2 - 1,) + down_block, BF),
            jax.ShapeDtypeStruct(gate_block, F32),
            jax.ShapeDtypeStruct((reps // 2 - 1,) + gate_block, BF),
        ),
        in_specs=[HBM, VMEM, VMEM, VMEM, HBM, HBM],
        out_specs=(VMEM, HBM, VMEM, VMEM, VMEM, VMEM, VMEM),
        scratch_shapes=scatter_scratch(half, width)
        + [
            pltpu.VMEM((2, half, width), BF),
            pltpu.VMEM((half, width), F32),
            pltpu.VMEM((reps // 2,) + down_block, BF),
            pltpu.VMEM((reps // 2,) + down_block, BF),
            pltpu.VMEM((reps // 2,) + gate_block, BF),
            pltpu.VMEM((reps // 2,) + gate_block, BF),
        ]
        + semaphores(4 * reps + SCATTER_COPIES + GATHER_COPIES, 4 * reps + 2),
        compiler_params=kernel_params(2),
        name="turn_back",
    )(
        parts.reshape(16, half, width), hidden, out_grad.reshape(2, half, width), gains,
        down_p, gate_p,
    )


def closing_kernel(
    layout, attn_p, up_p, out_p, gate_sum, one_parts, two_parts, tokens, hidden_grad, gains, vectors,
    query_back, key_back, value_back, swish_back, gate_back, up_back, out_sum, branch_two,
    tokens_grad, vector_sum,
    even_1, cores_1, taken_1, even_2, cores_2, taken_2, sum_buf, rows_buf, vec_l, vec_y,
    attn_l, attn_y, attn_s, up_l, up_y, up_s, out_l, out_y, send_sems, recv_sems, local_sems,
):
    links = Links(layout, send_sems, recv_sems, local_sems)
    device = links.device
    place, rep = layout.place(device), layout.rep(device)
    _, half, width = tokens.shape
    links.greet(layout.masks)
    backs, kept = [], []

    def place_at(mask):
        return layout.place(flip_device(device, mask)) if mask else place

    def give(source, target, mask):
        if mask:
            backs.append(links.send(source, target, mask))
        else:
            kept.append(links.local(source, target))

    edges, columns = 0, []
    for target in (query_back, key_back, value_back, swish_back):
        size = target.shape[1] // HEADS
        columns.append((target, size, edges))
        edges += size

    def with_return(item, mask, give_back):
        part, keep, taken, finish, paired = item

        def finish_and_give(value):
            finish(value)
            give_back(mask)

        return part, keep, taken, finish_and_give, paired

    def attn_return(mask):
        for target, size, at in columns:
            goal = pl.ds(pl.multiple_of(place * size, LANES), size)
            give(attn_s.at[place_at(mask), :, pl.ds(at, size)], target.at[:, goal], mask)

    def up_return(mask):
        give(up_s.at[place_at(mask)], up_back.at[place], mask)

    order = layout.team[::-1] + (0,)
    items = []
    for part, keep, taken, sums, give_back, paired in (
        (attn_p, attn_l, attn_y, attn_s, attn_return, False),
        (up_p, up_l, up_y, up_s, up_return, False),
    ):
        places = [place_at(m) for m in order]
        plain = replica_items(layout, rep, part, keep, taken, places, sums, paired)
        items += [with_return(item, m, give_back) for item, m in zip(plain, order)]
    items += replica_items(layout, rep, out_p, out_l, out_y, range(4), out_sum)
    steps = scatter_stream(links, items, 2, 2)

    pieces = layout.pieces(width)
    rows_buf[...] = jnp.zeros_like(rows_buf)
    rows_buf[2:4, :] = vectors[0:2, :]

    def finish_one(part, value):
        sum_buf[...] = value

        def rows(i, carry):
            at = pl.ds(pl.multiple_of(i * TILE, TILE), TILE)
            grads = from_weight_order(sum_buf[at, :], pieces)
            back, gain_part, shift_part = layer_norm_back(
                tokens[part, at, :].astype(F32), gains[0:1, :], grads
            )
            tokens_grad[part, at, :] = hidden_grad[part, at, :] + back
            rows_buf[0:1, :] += gain_part
            rows_buf[1:2, :] += shift_part
            return carry

        lax.fori_loop(0, half // TILE, rows, 0)

    def finish_two(part, value):
        branch_two[part] = value

    per = LANES // layout.shard
    own_bits = per.bit_length() - 1
    slots = layout.count // per
    flight = {}

    def vector_begin():
        for slot in range(slots):
            vec_l[slot] = rows_buf[:, slot * LANES : (slot + 1) * LANES]

    def vector_send(b):
        def run():
            peer = flip_device(device, 1 << b)
            if b >= own_bits:
                size = 1 << (b - own_bits)
                source = vec_l.at[pl.ds((peer // (1 << b)) * size, size)]
                target = vec_y.at[pl.ds(size, size)]
            else:
                source = vec_l.at[pl.ds(device // per, 1)]
                target = vec_y.at[pl.ds(slots + b, 1)]
            flight[b] = links.send(source, target, 1 << b)

        return run

    def vector_add(b):
        def run():
            if b >= own_bits:
                size = 1 << (b - own_bits)
                flight[b].wait_recv()
                mine = pl.ds((device // (1 << b)) * size, size)
                vec_l[mine] = vec_l[mine] + vec_y[size : 2 * size]
            else:
                links.swap_done(flight[b])
                mine = pl.ds(device // per, 1)
                vec_l[mine] = vec_l[mine] + vec_y[slots + b : slots + b + 1]

        return run

    def gate_return():
        for mask in layout.team + (0,):
            give(gate_sum.at[place_at(mask)], gate_back.at[place], mask)

    one = scatter_steps_light(links, one_parts, even_1, cores_1, taken_1, finish_one)
    two = scatter_steps_light(links, two_parts, even_2, cores_2, taken_2, finish_two)
    acts = one[1:] + [vector_begin]
    down_bits = list(range(layout.bits))[::-1]
    together = [(lambda b=b, a=a: ((a() if a else None), vector_send(b)())) for a, b in zip(
        [None] + [vector_add(b) for b in down_bits[:-1]], down_bits)]
    acts += [lambda: (together[0](), two[0](), gate_return())]
    for k in range(1, layout.bits):
        extra = two[k] if k < len(two) else (lambda: None)
        acts.append(lambda k=k, extra=extra: (together[k](), extra()))
    acts += two[layout.bits :] + [vector_add(down_bits[-1])]
    one[0]()
    interleave(steps, acts, 0)
    vector_sum[...] = vec_l[device // per]
    for copy in backs:
        copy.wait_recv()
    for copy in kept:
        copy.wait()
    links.finish()


def closing_call(layout, attn_p, up_p, out_p, gate_sum, one_parts, two_parts, tokens, hidden_grad,
                 gains, vectors, back_widths):
    reps, shard = layout.reps, layout.shard
    half, width = hidden_grad.shape[1:]
    attn_block, up_block, out_block = attn_p.shape[1:], up_p.shape[1:], out_p.shape[1:]
    per = LANES // shard
    slots = layout.count // per
    stay = reps // 2
    rows = jax.ShapeDtypeStruct((2, half, width), F32)
    copies = 20 * (reps - 1) + 7 * 6 + 2 * SCATTER_COPIES + layout.bits
    return pl.pallas_call(
        functools.partial(closing_kernel, layout),
        out_shape=tuple(jax.ShapeDtypeStruct((shard, w), BF) for w in back_widths)
        + (
            jax.ShapeDtypeStruct(up_block, BF),
            jax.ShapeDtypeStruct(up_block, BF),
            jax.ShapeDtypeStruct(out_block, F32),
            rows,
            rows,
            jax.ShapeDtypeStruct((8, LANES), F32),
        ),
        in_specs=[HBM, HBM, HBM, VMEM, HBM, HBM, VMEM, VMEM, VMEM, VMEM],
        out_specs=(HBM,) * 6 + (VMEM,) * 4,
        scratch_shapes=scatter_scratch(half, width)
        + scatter_scratch(half, width)
        + [
            pltpu.VMEM((half, width), F32),
            pltpu.VMEM((8, width), F32),
            pltpu.VMEM((slots, 8, LANES), F32),
            pltpu.VMEM((slots + per, 8, LANES), F32),
            pltpu.VMEM((stay,) + attn_block, BF),
            pltpu.VMEM((reps - 1,) + attn_block, BF),
            pltpu.VMEM(attn_block, BF),
            pltpu.VMEM((stay,) + up_block, BF),
            pltpu.VMEM((reps - 1,) + up_block, BF),
            pltpu.VMEM(up_block, BF),
            pltpu.VMEM((stay,) + out_block, BF),
            pltpu.VMEM((reps - 1,) + out_block, BF),
        ]
        + semaphores(copies, 20 * stay + 8),
        compiler_params=kernel_params(3),
        name="closing",
    )(
        attn_p, up_p, out_p, gate_sum, one_parts.reshape(16, half, width),
        two_parts.reshape(16, half, width), tokens.reshape(2, half, width), hidden_grad, gains, vectors,
    )


def seq_layout(seq_lens, row_count):
    row_ids = jnp.arange(row_count, dtype=jnp.int32)
    seq_ends = jnp.cumsum(seq_lens)
    passed = row_ids[:, None] >= seq_ends[None, :]
    segment = jnp.sum(passed.astype(jnp.int32), axis=1)
    seq_start = jnp.sum(jnp.where(passed, seq_lens[None, :], 0), axis=1)
    position = row_ids - seq_start
    live_rows = row_ids < seq_ends[-1]
    return (segment, position, live_rows)


def group_norm(values):
    center = values - jnp.mean(values, axis=-1, keepdims=True)
    spread = jnp.mean(center * center, axis=-1, keepdims=True)
    return center * lax.rsqrt(spread + GROUP_EPS)


def dot(left, right):
    return jnp.dot(left, right, preferred_element_type=F32)


def dot_nt(left, right):
    return lax.dot_general(left, right, (((1,), (1,)), ((), ())), preferred_element_type=F32)


def dot_tn(left, right):
    return lax.dot_general(left, right, (((0,), (0,)), ((), ())), preferred_element_type=F32)


def make_body(count):
    def on_device(
        tokens,
        seq_lengths,
        attn_gain,
        attn_shift,
        query_weight,
        key_weight,
        value_weight,
        gate_weight,
        out_weight,
        mlp_gain,
        mlp_shift,
        mlp_gate,
        mlp_up,
        mlp_down,
        cotangent,
    ):
        local_rows, width = tokens.shape
        shard = width // count
        layout = Layout(count, shard)
        reps = layout.reps
        device = lax.axis_index("dp")
        rep, pos_t = layout.rep(device), layout.place(device)
        micro_count, seq_slots = seq_lengths.shape[1:]
        row_count = local_rows // micro_count
        key_size = query_weight.shape[1] // HEADS
        value_size = value_weight.shape[1] // HEADS
        hidden_size = mlp_gate.shape[1]
        ff_block = hidden_size // count
        group_rows = 8 * local_rows
        home = [layout.device(d % reps, d // reps) for d in range(count)]
        head_perm = [(d, home[d]) for d in range(count)]
        head_back = [(b, a) for a, b in head_perm]

        high, mid = 1 << (layout.bits - 1 - layout.far_bit), 1 << (layout.far_bit - 2)

        def ff_first(weight):
            v = weight.reshape(shard, high, 2, mid, 4, ff_block)
            return v.transpose(2, 4, 0, 1, 3, 5).reshape(8, shard, reps * ff_block)

        def ff_back(grad):
            v = grad.reshape(2, 4, shard, high, mid, ff_block)
            return v.transpose(2, 3, 0, 4, 1, 5).reshape(shard, hidden_size)

        per = LANES // shard
        lane_on = jnp.arange(LANES, dtype=jnp.int32) // shard == device % per

        def in_lanes(values):
            return jnp.where(lane_on, jnp.tile(values, per), jnp.zeros((), BF))[None]

        own_lens = seq_lengths.reshape(-1).astype(BF)
        small = jnp.concatenate(
            [in_lanes(v) for v in (attn_gain, attn_shift, mlp_gain, mlp_shift)]
            + [jnp.pad(own_lens, (0, LANES - own_lens.shape[0]))[None], jnp.zeros((3, LANES), BF)]
        )
        own_live = jax.vmap(lambda v: seq_layout(v, row_count)[2])(seq_lengths[0])
        own_live = own_live.reshape(local_rows).astype(F32)[:, None]
        out_grad_low = (cotangent.astype(F32) * own_live).astype(BF)

        out_own = lax.ppermute(out_weight, "dp", head_perm)
        small, normed_one, cot_all, attn_w, gate_in, up_in, out_w = opening_call(
            layout, small[None], tokens, out_grad_low,
            (query_weight, key_weight, value_weight, gate_weight),
            ff_first(mlp_gate), ff_first(mlp_up), out_own,
        )
        normed_one = normed_one.reshape(group_rows, width)
        cot_all = cot_all.reshape(group_rows, width)
        attn_w = attn_w.reshape(width, -1)
        out_w = out_w.reshape(-1, width)

        def flip_rep(values, bit):
            mask = 1 << layout.rep_bits[bit]
            return lax.ppermute(values, "dp", [(d, d ^ mask) for d in range(count)])

        down_even = [lax.optimization_barrier((mlp_down, small))[0]]
        for k in range(1, reps // 2):
            low = layout.low(k)
            down_even.append(flip_rep(down_even[k & ~(1 << low)], low + 1))

        def finish_pairs(first, rest):
            sums = [first] + [rest[k] for k in range(reps // 2 - 1)]
            for k in range(reps // 2 - 1, 0, -1):
                low = layout.low(k)
                got = flip_rep(sums[k].astype(BF), low + 1).astype(F32)
                sums[k & ~(1 << low)] = sums[k & ~(1 << low)].astype(F32) + got
            return sums[0]

        vecs = small[:, :4, :].astype(F32).reshape(-1, per, 4, LANES).sum(1)
        vecs = vecs.transpose(1, 0, 2).reshape(4, width)
        gains_one = jnp.pad(vecs[:2], ((0, 6), (0, 0)))
        gains_two = jnp.pad(vecs[2:], ((0, 6), (0, 0)))
        lens = small[:, 4, : own_lens.shape[0]].astype(jnp.int32)
        order = [c + 2 * n + 4 * f for c in range(2) for f in range(2) for n in range(2)]
        members = jnp.stack(
            [flip_device(device, (j & 3) + (j >> 2) * layout.far) for j in order]
        )
        lens = jnp.take(lens, members, axis=0).reshape(8 * micro_count, seq_slots)

        segment, position, live = jax.vmap(lambda s: seq_layout(s, row_count))(lens)
        head_log = jnp.log(1.0 - 2.0 ** (-5.0 - jnp.arange(HEADS, dtype=F32)))
        head_log = lax.dynamic_index_in_dim(head_log, pos_t, 0, keepdims=False)
        ids = jnp.arange(row_count, dtype=jnp.int32)
        same_seq = (
            (segment[:, :, None] == segment[:, None, :])
            & live[:, :, None]
            & live[:, None, :]
            & (ids[:, None] >= ids[None, :])[None]
        )
        distance = jnp.maximum(position[:, :, None] - position[:, None, :], 0).astype(F32)
        decay = jnp.where(same_seq, jnp.exp(distance * head_log), 0.0)
        half_size = key_size // 2
        pair_index = jnp.arange(half_size, dtype=F32)
        frequency = 10000.0 ** (-pair_index / half_size)
        row_place = position.reshape(-1).astype(F32)[:, None]
        angles = row_place * frequency[None, :]
        growth = (pair_index * 2.0 / key_size + 0.4) / 1.4
        stretch = growth[None, :] ** (row_place / 512.0)
        key_factor = key_size ** (-0.5) / stretch
        cosine, sine, stretch, key_factor = lax.optimization_barrier(
            (jnp.cos(angles), jnp.sin(angles), stretch, key_factor)
        )

        def rotate(values, factor):
            a, b = values[:, :half_size], values[:, half_size:]
            return jnp.concatenate(
                [(a * cosine - b * sine) * factor, (b * cosine + a * sine) * factor], axis=1
            )

        def rotate_back(grads, factor):
            a, b = grads[:, :half_size] * factor, grads[:, half_size:] * factor
            return jnp.concatenate([a * cosine + b * sine, b * cosine - a * sine], axis=1)

        def micro(values):
            return values.reshape(-1, row_count, values.shape[-1])

        qkvg = dot(normed_one, attn_w)
        query_raw = qkvg[:, :key_size]
        key_raw = qkvg[:, key_size : 2 * key_size]
        value_low = qkvg[:, 2 * key_size : 2 * key_size + value_size].astype(BF)
        gate_raw = qkvg[:, 2 * key_size + value_size :]
        query_turned = micro(rotate(query_raw, stretch).astype(BF))
        key_turned = micro(rotate(key_raw, key_factor).astype(BF))
        value_m = micro(value_low)
        scores = jnp.einsum("mqd,mkd->mqk", query_turned, key_turned, preferred_element_type=F32)
        weights_low = (scores * decay).astype(BF)
        retained = jnp.einsum("mqk,mke->mqe", weights_low, value_m, preferred_element_type=F32)
        retained = retained.reshape(group_rows, value_size)

        def mix(gate_in, retained_in):
            return jax.nn.silu(gate_in) * group_norm(retained_in)

        mixed = mix(gate_raw, retained).astype(BF)
        hidden, normed_two, gate_w, up_w, down_w = turn_call(
            layout, dot(mixed, out_w).astype(BF), tokens, gains_two, gate_in, up_in,
            jnp.stack(down_even),
        )
        down_w = down_w.reshape(-1, width)
        normed_two = normed_two.reshape(group_rows, width)
        gate_w, up_w = gate_w.reshape(width, -1), up_w.reshape(width, -1)

        def act(gate_in, up_in):
            return jax.nn.gelu(gate_in, approximate=True) * up_in

        product, pull_act = jax.vjp(act, dot(normed_two, gate_w), dot(normed_two, up_w))
        product = product.astype(BF)
        gate_low, up_low = (g.astype(BF) for g in pull_act(dot_nt(cot_all, down_w)))
        two_parts = dot(product, down_w).astype(BF)
        down_parts = dot_tn(product, cot_all).astype(BF)
        gate_parts = dot_tn(normed_two, gate_low).astype(BF)
        up_parts = dot_tn(normed_two, up_low).astype(BF)
        normed_parts = (dot_nt(gate_low, gate_w) + dot_nt(up_low, up_w)).astype(BF)
        hidden_grad, branch_one_grad, vectors, down_first, down_rest, gate_first, gate_rest = turn_back_call(
            layout, normed_parts, hidden, out_grad_low, gains_two,
            down_parts.reshape(reps, 4, -1, width), gate_parts.reshape(reps, 8, shard, -1),
        )
        branch_one_grad = branch_one_grad.reshape(group_rows, width)
        gate_sum = finish_pairs(gate_first, gate_rest).astype(BF)
        mlp_down_grad = finish_pairs(down_first, down_rest)

        mixed_grad = dot_nt(branch_one_grad, out_w)
        _, pull_mix = jax.vjp(mix, gate_raw, retained)
        gate_grad, retained_grad = pull_mix(mixed_grad)
        gate_grad = gate_grad.astype(BF)
        retained_low = micro(retained_grad.astype(BF))
        weights_grad = jnp.einsum("mqe,mke->mqk", retained_low, value_m, preferred_element_type=F32)
        value_grad = jnp.einsum(
            "mqk,mqe->mke", weights_low, retained_low, preferred_element_type=F32
        )
        value_grad = value_grad.reshape(group_rows, value_size).astype(BF)
        score_low = (weights_grad * decay).astype(BF)
        query_turn_grad = jnp.einsum("mqk,mkd->mqd", score_low, key_turned, preferred_element_type=F32)
        key_turn_grad = jnp.einsum("mqk,mqd->mkd", score_low, query_turned, preferred_element_type=F32)
        query_grad = rotate_back(query_turn_grad.reshape(group_rows, key_size), stretch).astype(BF)
        key_grad = rotate_back(key_turn_grad.reshape(group_rows, key_size), key_factor).astype(BF)
        attn_grads = jnp.concatenate([query_grad, key_grad, value_grad, gate_grad], axis=1)
        attn_parts = dot_tn(normed_one, attn_grads).astype(BF)
        out_parts = dot_tn(mixed, branch_one_grad).astype(BF)
        one_parts = dot_nt(attn_grads, attn_w).astype(BF)
        q_back, k_back, v_back, g_back, gate_back, up_back, out_sum, branch_two, tokens_grad, vectors = (
            closing_call(
                layout,
                attn_parts.reshape(reps, 8, shard, -1),
                up_parts.reshape(reps, 8, shard, -1),
                out_parts.reshape(reps, 4, -1, width),
                gate_sum, one_parts, two_parts, tokens, hidden_grad, gains_one, vectors,
                [w.shape[1] for w in (query_weight, key_weight, value_weight, gate_weight)],
            )
        )
        out_sum = out_sum.reshape(out_weight.shape).astype(BF)
        out_weight_grad = lax.ppermute(out_sum, "dp", head_back).astype(F32)
        output = ((hidden + branch_two).reshape(local_rows, width) * own_live).astype(BF)
        vectors = lax.dynamic_slice_in_dim(vectors, (device % per) * shard, shard, axis=1)
        return (
            output,
            tokens_grad.reshape(local_rows, width),
            vectors[0],
            vectors[1],
            q_back.astype(F32),
            k_back.astype(F32),
            v_back.astype(F32),
            g_back.astype(F32),
            out_weight_grad,
            vectors[2],
            vectors[3],
            ff_back(gate_back.astype(F32)),
            ff_back(up_back.astype(F32)),
            mlp_down_grad.reshape(mlp_down.shape),
        )

    return on_device


def solution(mesh):
    rows = P("dp", None)
    vec = P("dp")
    placed = (
        rows, P("dp", None, None), vec, vec, rows, rows, rows, rows, rows,
        vec, vec, rows, rows, rows, rows,
    )
    outs = (rows, rows, vec, vec, rows, rows, rows, rows, rows, vec, vec, rows, rows, rows)
    return jax.shard_map(
        make_body(mesh.shape["dp"]), mesh=mesh, in_specs=placed, out_specs=outs, check_vma=False
    )
```

profile of v0, /device:TPU:0, one launch (start us, length us, event | category | flops | bytes accessed | tf_op | source)
XLA Modules:
  0.0 598.2 jit_solution(4317060802472970197)
XLA Ops:
  0.7 1.8 collective-permute-start
  2.6 0.7 tile.16
  3.3 0.7 tile.18
  4.0 0.7 tile.40
  4.8 0.7 tile.42
  5.7 0.9 fusion.28
  7.1 1.4 reshape.794
  8.9 1.0 reshape.795.gate_src
  10.7 1.0 reshape.797.up_src
  12.9 0.9 multiply_convert_fusion.3
  13.8 0.8 copy-done.28
  14.6 134.4 %opening.1 = (bf16[32,8,128]{2,1,0:T(8,128)(2,1)}, bf16[16,64,2048]{2,1,0:T(8,128)(2,1)}, bf16[16,64,2048]{2,1,0:T(8,128)(2,1)}, bf16[4,8,64,1536]{3,2,1,0:T(8,1...) custom-call(bf16[1,8,128]{2,1,0:T(8,128)(2,1)} %bitcast.177, ...), custom_call_target="tpu_custom_call" | custom-call | tf_op jit(solution)/shard_map/opening/pallas_call | solution.py:610
  149.1 0.9 slice_convert_fusion.1
  150.0 0.9 convert_reduce_fusion
  152.3 1.9 multiply_sine_fusion
  154.2 1.4 power_multiply_fusion
  155.6 10.4 %fusion.30 = f32[1024,1536]{1,0:T(8,128)S(1)} fusion(bf16[1024,2048]{1,0:T(8,128)(2,1)} %bitcast.182, bf16[2048,1536]{1,0:T(8,128)(2,1)} %bitcast.178), kind=kOutput, calls=%fused_computation.125 | convolution fusion | flops 6442450944 | bytes 16777216 | tf_op jit(solution)/shard_map/dot_general | solution.py:1041
  166.6 2.1 copy-done
  168.7 1.7 fusion.11
  171.6 2.6 multiply_convert_fusion.2
  174.3 0.7 pad.13.gains
  175.6 4.4 convolution_convert_fusion.3
  180.0 2.3 pad_maximum_fusion.down_in
  182.3 77.3 %turn.1 = (f32[2,64,2048]{2,1,0:T(8,128)}, bf16[16,64,2048]{2,1,0:T(8,128)(2,1)}, bf16[4,8,64,512]{3,2,1,0:T(8,128)(2,1)}, bf16[4,8,64,512]{3,2,1,0:T(8,128)(2,1)}, bf16[4,128,2048]{2,1,0:T(8,128)(2,1)}) custom-call(bf16[16,64,2048]{2,1,0:T(8,128)(2,1)} %bitcast.150, bf16[2,64,2048]{2,1,0:T(8,128)(2,1)} %bitcast.145, f32[8,2048]{1,0:T(8,128)} %pad.12.gains, ...), custom_call_target="tpu_custom_call" | custom-call | tf_op jit(solution)/shard_map/turn/pallas_call | solution.py:698
  259.6 5.3 fusion.32
  265.0 2.3 fusion.31
  267.8 3.9 multiply_convert_fusion
  271.7 3.9 convolution_convert_fusion.6
  275.6 2.4 fusion.33
  277.9 4.0 convolution_convert_fusion.7
  281.9 3.8 convolution_convert_fusion.5
  285.7 4.4 add_convert_fusion
  290.1 60.0 %turn_back.1 = (f32[2,64,2048]{2,1,0:T(8,128)}, bf16[16,64,2048]{2,1,0:T(8,128)(2,1)}, f32[8,2048]{1,0:T(8,128)}, f32[4,32,2048]{2,1,0:T(8,128)}, bf16[1,4,32,20...) custom-call(bf16[16,64,2048]{2,1,0:T(8,128)(2,1)} %bitcast.149, ...), custom_call_target="tpu_custom_call" | custom-call | tf_op jit(solution)/shard_map/turn_back/pallas_call | solution.py:801
  350.2 6.3 %multiply_reduce_fusion = (f32[1024]{0:T(1024)S(1)}, f32[1024,512]{1,0:T(8,128)S(1)}) fusion(f32[16,64,512]{2,1,0:T(8,128)S(1)} %get-tuple-element.113, f32[1024]{0:T(1024)S(1)} %div.109, f32[1024,1536]{1,0:T(8,128)} %copy-done, bf16[1024,2048]{1,0:T(8,128)(2,1)} %bitcast.186, bf16[512,2048]{1,0:T(8,128)(2,1)} %bitcast.192), kind=kOutput, calls=%fused_computation.27 | convolution fusion | flops 2151676928 | bytes 12591104 | tf_op jit(solution)/shard_map/dot_general | solution.py:1045
  356.5 3.3 fusion.27
  360.0 1.0 copy-done.7
  361.0 1.6 fusion.12
  364.6 0.8 copy-done.2
  366.1 8.3 %convolution_convert_fusion.1 = bf16[1024,2048]{1,0:T(8,128)(2,1)} fusion(bf16[1024,1536]{1,0:T(8,128)(2,1)S(1)} %constant_dynamic-update-slice_fusion, bf16[2048,1536]{1,0:T(8,128)(2,1)S(1)} %bitcast.181), kind=kOutput, calls=%fused_computation.3 | convolution fusion | flops 6444548096 | bytes 13631488 | tf_op jit(solution)/shard_map/dot_general | solution.py:1045
  374.4 8.7 %convolution_convert_fusion = bf16[2048,1536]{1,0:T(8,128)(2,1)} fusion(bf16[1024,2048]{1,0:T(8,128)(2,1)S(1)} %bitcast.183, bf16[1024,1536]{1,0:T(8,128)(2,1)S(1)} %constant_dynamic-update-slice_fusion), kind=kOutput, calls=%fused_computation.2 | convolution fusion | flops 6445596672 | bytes 13631488 | tf_op jit(solution)/shard_map/dot_general | solution.py:1049
  383.1 2.0 collective-permute-start.2
  385.1 3.8 convolution_convert_fusion.4
  388.9 1.0 collective-permute-start.4
  389.9 4.4 convolution_convert_fusion.2
  394.3 26.0 %collective-permute-done.2 = bf16[8,64,512]{2,1,0:T(8,128)(2,1)S(1)} collective-permute-done((bf16[8,64,512]{2,1,0:T(8,128)(2,1)S(1)}, bf16[8,64,512]{2,1,0:T(8,128)(2,1)S(1)}, u32[]{:S(2)}, u32[]{:S(2)}) %collective-permute-start.2) | collective-permute-done | bytes 524320 | tf_op jit(solution)/shard_map/ppermute | solution.py:1125
  420.3 1.0 add_convert_fusion.2.gate_sum
  421.2 152.7 %closing.1 = (bf16[64,2048]{1,0:T(8,128)(2,1)}, bf16[64,2048]{1,0:T(8,128)(2,1)}, bf16[64,4096]{1,0:T(8,128)(2,1)}, bf16[64,4096]{1,0:T(8,128)(2,1)}, bf16[8,64,...) custom-call(bf16[4,8,64,1536]{3,2,1,0:T(8,128)(2,1)} %bitcast.141, ...), custom_call_target="tpu_custom_call" | custom-call | tf_op jit(solution)/shard_map/closing/pallas_call | solution.py:985
  573.9 1.4 add.196
  575.4 0.9 fusion.13
  576.3 0.9 convert_element_type.190
  577.2 5.4 collective-permute-start.3
  583.2 0.8 convert_element_type.186
  584.0 0.8 convert_element_type.187
  584.8 1.0 convert_element_type.188
  585.9 1.0 convert_element_type.189
  586.9 0.6 reshape.844
  587.6 0.7 copy.53
  588.3 1.4 reshape.838
  589.7 0.6 reshape.846
  590.3 0.7 copy.54
  591.0 1.4 reshape.840
  592.4 2.2 convert_add_fusion
  594.7 2.1 convert_element_type.192
  596.8 1.0 copy.67
  (158 shorter events, 11.4 us)
Async XLA Ops:
  0.6 9.3 %copy-start.26 = (bf16[64,4096]{1,0:T(8,128)(2,1)S(1)}, bf16[64,4096]{1,0:T(8,128)(2,1)}, u32[]{:S(2)}) copy-start(bf16[64,4096]{1,0:T(8,128)(2,1)} %param.27) | copy-start | bytes 1572868
  0.7 13.2 %collective-permute-start = (bf16[128,2048]{1,0:T(8,128)(2,1)}, bf16[128,2048]{1,0:T(8,128)(2,1)S(1)}, u32[]{:S(2)}, u32[]{:S(2)}) collective-permute-start(bf16[128,2048]{1,0:T(8,128)(2,1)} %param.23), channel_id=1, source_target_pairs={{0,0},{1,4},{2,16},{3,20},{4,1},{5,5},{6,17},{7,21},{8,2},{9,6},{1... | collective-permute-start | bytes 1572872 | tf_op jit(solution)/shard_map/ppermute | solution.py:1112
  8.9 4.0 copy-start.27
  13.8 0.8 copy-start.28
  152.3 27.7 %collective-permute-start.1 = (bf16[128,2048]{1,0:T(8,128)(2,1)}, bf16[128,2048]{1,0:T(8,128)(2,1)}, u32[]{:S(2)}, u32[]{:S(2)}) collective-permute-start(bf16[128,2048]{1,0:T(8,128)(2,1)} %param.28), channel_id=1, source_target_pairs={{0,16},{1,17},{2,18},{3,19},{4,20},{5,21},{6,22},{7,23},{8,24},{9,... | collective-permute-start | bytes 1572872 | tf_op jit(solution)/shard_map/ppermute | solution.py:1125
  155.6 10.6 %copy-start.1 = (f32[1024,128]{1,0:T(8,128)}, f32[1024,128]{1,0:T(8,128)S(1)}, u32[]{:S(2)}) copy-start(f32[1024,128]{1,0:T(8,128)S(1)} %get-tuple-element.54) | copy-start | bytes 1572868
  155.6 10.6 %copy-start.3 = (f32[1024,128]{1,0:T(8,128)}, f32[1024,128]{1,0:T(8,128)S(1)}, u32[]{:S(2)}) copy-start(f32[1024,128]{1,0:T(8,128)S(1)} %get-tuple-element.53) | copy-start | bytes 1572868
  166.0 2.7 copy-start
  166.2 4.2 copy-start.6
  168.6 1.7 copy-start.10
  168.7 1.7 copy-start.12
  168.7 1.7 copy-start.14
  170.3 0.7 copy-start.20
  171.6 4.0 copy-start.36
  174.3 5.7 copy-start.8
  259.6 5.3 copy-start.35
  259.6 5.3 copy-start.39
  265.0 2.3 copy-start.33
  265.0 2.9 copy-start.37
  271.7 6.3 %copy-start.42 = (bf16[1024,512]{1,0:T(8,128)(2,1)}, bf16[1024,512]{1,0:T(8,128)(2,1)S(1)}, u32[]{:S(2)}) copy-start(bf16[1024,512]{1,0:T(8,128)(2,1)S(1)} %get-tuple-element.93) | copy-start | bytes 3145732
  271.7 3.9 copy-start.40
  356.5 9.6 %slice-start = ((s8[6291456]{0:T(1024)(128)(4,1)}), s8[4194304]{0:T(1024)(128)(4,1)S(1)}, s32[]{:S(2)}) async-start(s8[6291456]{0:T(1024)(128)(4,1)} %bitcast.179), calls=%async_computation | async-start | bytes 8388608
  359.8 1.2 copy-start.7
  360.0 2.6 copy-start.21
  361.0 2.1 copy-start.13
  361.0 2.1 copy-start.15
  362.6 1.0 copy-start.11
  363.1 1.1 copy-start.4
  363.2 2.9 slice-start.1
  364.4 1.0 copy-start.2
  366.1 8.3 %copy-start.32 = (bf16[16,64,2048]{2,1,0:T(8,128)(2,1)S(1)}, bf16[16,64,2048]{2,1,0:T(8,128)(2,1)}, u32[]{:S(2)}) copy-start(bf16[16,64,2048]{2,1,0:T(8,128)(2,1)} %get-tuple-element.48) | copy-start | bytes 12582916
  374.4 8.7 %copy-start.41 = (bf16[1,8,64,512]{3,2,1,0:T(8,128)(2,1)S(1)}, bf16[1,8,64,512]{3,2,1,0:T(8,128)(2,1)}, u32[]{:S(2)}) copy-start(bf16[1,8,64,512]{3,2,1,0:T(8,128)(2,1)} %get-tuple-element.67) | copy-start | bytes 1572868
  374.4 10.7 %copy-start.9 = (bf16[1024,512]{1,0:T(8,128)(2,1)S(1)}, bf16[1024,512]{1,0:T(8,128)(2,1)}, u32[]{:S(2)}) copy-start(bf16[1024,512]{1,0:T(8,128)(2,1)} %copy-done.8) | copy-start | bytes 3145732
  374.4 10.7 %copy-start.34 = (bf16[16,64,2048]{2,1,0:T(8,128)(2,1)S(1)}, bf16[16,64,2048]{2,1,0:T(8,128)(2,1)}, u32[]{:S(2)}) copy-start(bf16[16,64,2048]{2,1,0:T(8,128)(2,1)} %get-tuple-element.65) | copy-start | bytes 12582916
  383.1 6.8 %copy-start.38 = (bf16[4,128,2048]{2,1,0:T(8,128)(2,1)S(1)}, bf16[4,128,2048]{2,1,0:T(8,128)(2,1)}, u32[]{:S(2)}) copy-start(bf16[4,128,2048]{2,1,0:T(8,128)(2,1)} %get-tuple-element.61) | copy-start | bytes 6291460
  383.1 6.8 %copy-start.43 = (bf16[1024,512]{1,0:T(8,128)(2,1)S(1)}, bf16[1024,512]{1,0:T(8,128)(2,1)}, u32[]{:S(2)}) copy-start(bf16[1024,512]{1,0:T(8,128)(2,1)} %copy-done.42) | copy-start | bytes 3145732
  383.1 37.2 %collective-permute-start.2 = (bf16[8,64,512]{2,1,0:T(8,128)(2,1)S(1)}, bf16[8,64,512]{2,1,0:T(8,128)(2,1)S(1)}, u32[]{:S(2)}, u32[]{:S(2)}) collective-permute-start(bf16[8,64,512]{2,1,0:T(8,128)(2,1)S(1)} %bitcast.200), channel_id=1, source_target_pairs={{0,16},{1,17},{2,18},{3,19},{4,20},{5,21},{6,22},{7,23},{8,24},{9,... | collective-permute-start | bytes 1572872 | tf_op jit(solution)/shard_map/ppermute | solution.py:1125
  388.9 31.4 %copy-start.18 = (f32[8,64,512]{2,1,0:T(8,128)S(1)}, f32[8,64,512]{2,1,0:T(8,128)}, u32[]{:S(2)}) copy-start(f32[8,64,512]{2,1,0:T(8,128)} %get-tuple-element.66) | copy-start | bytes 3145732
  388.9 203.5 %collective-permute-start.4 = (bf16[4,32,2048]{2,1,0:T(8,128)(2,1)}, bf16[4,32,2048]{2,1,0:T(8,128)(2,1)}, u32[]{:S(2)}, u32[]{:S(2)}) collective-permute-start(bf16[4,32,2048]{2,1,0:T(8,128)(2,1)} %bitcast.70), channel_id=1, source_target_pairs={{0,16},{1,17},{2,18},{3,19},{4,20},{5,21},{6,22},{7,23},{8,24},{9,... | collective-permute-start | bytes 1572872 | tf_op jit(solution)/shard_map/ppermute | solution.py:1125
  421.2 152.7 %copy-start.5 = (f32[2,64,2048]{2,1,0:T(8,128)S(1)}, f32[2,64,2048]{2,1,0:T(8,128)}, u32[]{:S(2)}) copy-start(f32[2,64,2048]{2,1,0:T(8,128)} %get-tuple-element.59.hidden) | copy-start | bytes 3145732
  573.9 2.4 copy-start.16
  575.4 7.2 %copy-start.31 = (f32[8,128]{1,0:T(8,128)S(1)}, f32[8,128]{1,0:T(8,128)}, u32[]{:S(2)}) copy-start(f32[8,128]{1,0:T(8,128)} %get-tuple-element.72) | copy-start | bytes 12292
  575.4 7.8 %copy-start.30 = (bf16[64,2048]{1,0:T(8,128)(2,1)S(1)}, bf16[64,2048]{1,0:T(8,128)(2,1)}, u32[]{:S(2)}) copy-start(bf16[64,2048]{1,0:T(8,128)(2,1)} %get-tuple-element.73) | copy-start | bytes 786436
  575.4 8.6 %copy-start.29 = (bf16[64,2048]{1,0:T(8,128)(2,1)S(1)}, bf16[64,2048]{1,0:T(8,128)(2,1)}, u32[]{:S(2)}) copy-start(bf16[64,2048]{1,0:T(8,128)(2,1)} %get-tuple-element.74) | copy-start | bytes 786436
  575.4 9.4 %copy-start.25 = (bf16[64,4096]{1,0:T(8,128)(2,1)S(1)}, bf16[64,4096]{1,0:T(8,128)(2,1)}, u32[]{:S(2)}) copy-start(bf16[64,4096]{1,0:T(8,128)(2,1)} %get-tuple-element.75) | copy-start | bytes 1572868
  576.3 9.5 %copy-start.24 = (bf16[64,4096]{1,0:T(8,128)(2,1)S(1)}, bf16[64,4096]{1,0:T(8,128)(2,1)}, u32[]{:S(2)}) copy-start(bf16[64,4096]{1,0:T(8,128)(2,1)} %get-tuple-element.76) | copy-start | bytes 1572868
  577.2 17.4 %collective-permute-start.3 = (bf16[128,2048]{1,0:T(8,128)(2,1)}, bf16[128,2048]{1,0:T(8,128)(2,1)}, u32[]{:S(2)}, u32[]{:S(2)}) collective-permute-start(bf16[128,2048]{1,0:T(8,128)(2,1)} %bitcast.65), channel_id=1, source_target_pairs={{0,0},{4,1},{16,2},{20,3},{1,4},{5,5},{17,6},{21,7},{2,8},{6,9},{1... | collective-permute-start | bytes 1572872 | tf_op jit(solution)/shard_map/ppermute | solution.py:1262
  584.0 2.9 copy-start.23
  587.6 2.1 copy-start.22
  590.3 2.1 copy-start.17
  592.4 4.4 copy-start.19
where the time goes:
time: 607 us; the launch traced here: 598 us
  Pallas kernels  424 us (70%)
  matrix products  81 us (13%)
  other arithmetic  29.8 us (5%)
  waiting for transfers between devices  26 us (4%)
  local copies, waits for them, and re-layouts  25 us (4%)
  starting transfers between devices  10.1 us (2%)
    pallas_call x1, Pallas kernels, closing_call(): pl.pallas_call(functools.partial(closing_kernel, layout), out_shape=tuple...  153 us
    pallas_call x1, Pallas kernels, opening_call(): pl.pallas_call(functools.partial(opening_kernel, layout), out_shape=(jax....  134 us
    pallas_call x1, Pallas kernels, turn_call(): pl.pallas_call(functools.partial(turn_kernel, layout), out_shape=(jax.Sha...  77.3 us
    pallas_call x1, Pallas kernels, turn_back_call(): pl.pallas_call(functools.partial(turn_back_kernel, layout), out_shape=(ja...  60 us
    dot_general x5, matrix products, dot(): return jnp.dot(left, right, preferred_element_type=F32)  26.8 us
    ppermute x3, waiting for transfers between devices, flip_rep(): return lax.ppermute(values, 'dp', [(d, d ^ mask) for d in range(count)])  26 us
    dot_general x5, matrix products, dot_nt(): lax.dot_general(left, right, (((1,), (1,)), ((), ())), preferred_element_...  25.2 us
    dot_general x5, matrix products, dot_tn(): lax.dot_general(left, right, (((0,), (0,)), ((), ())), preferred_element_...  24.1 us
  transfers between devices with their start and end apart: 5, of which 1 were waited for; matrix products, arithmetic and copies ran while one was open for 10% of the time, Pallas kernels for 26%

commit v1 on v0

--- a/solution.py
+++ b/solution.py
@@ -434,6 +434,14 @@
         return run
 
     return [step(k) for k in range(len(items) + window)]
+
+
+def both(first, second):
+    def run():
+        first()
+        second()
+
+    return run
 
 
 def interleave(stream, acts, first=1):
@@ -718,9 +726,9 @@
 
 
 def turn_back_kernel(
-    layout, parts, hidden, out_grad, gains, down_p, gate_p,
-    hidden_grad, all_rows, vectors, down_first, down_rest, gate_first, gate_rest,
-    even, cores, taken, low_buf, sum_buf, down_l, down_y, gate_l, gate_y,
+    layout, parts, hidden, out_grad, gains, down_p, gate_p, up_p,
+    hidden_grad, all_rows, vectors, down_sum, gate_sum, up_first, up_rest,
+    even, cores, taken, low_buf, sum_buf, down_l, down_y, gate_l, gate_y, up_l, up_y,
     send_sems, recv_sems, local_sems,
 ):
     links = Links(layout, send_sems, recv_sems, local_sems)
@@ -743,9 +751,12 @@
         )
 
     pairs = [pl.ds(2 * part, 2) for part in range(4)]
-    items = [item(down_p, down_l, down_y, at, down_first, down_rest) for at in range(4)]
-    items += [item(gate_p, gate_l, gate_y, at, gate_first, gate_rest) for at in pairs]
-    steps = pair_stream(links, items, 3)
+    items = replica_items(layout, rep, down_p, down_l, down_y, range(4), down_sum)
+    items += replica_items(layout, rep, gate_p, gate_l, gate_y, pairs, gate_sum)
+    steps = scatter_stream(links, items, 2, 2)
+    late = pair_stream(links, [item(up_p, up_l, up_y, at, up_first, up_rest) for at in pairs], 2)
+    for k, more in enumerate(late):
+        steps[min(k + 5, 11)] = both(steps[min(k + 5, 11)], more)
     pieces = layout.pieces(width)
     vectors[...] = jnp.zeros_like(vectors)
 
@@ -794,7 +805,7 @@
     return [item(at) for at in places]
 
 
-def turn_back_call(layout, parts, hidden, out_grad, gains, down_p, gate_p):
+def turn_back_call(layout, parts, hidden, out_grad, gains, down_p, gate_p, up_p):
     half, width = hidden.shape[1:]
     reps = layout.reps
     down_block, gate_block = down_p.shape[1:], gate_p.shape[1:]
@@ -805,36 +816,40 @@
             jax.ShapeDtypeStruct((16, half, width), BF),
             jax.ShapeDtypeStruct((8, width), F32),
             jax.ShapeDtypeStruct(down_block, F32),
-            jax.ShapeDtypeStruct((reps // 2 - 1,) + down_block, BF),
+            jax.ShapeDtypeStruct(gate_block, BF),
             jax.ShapeDtypeStruct(gate_block, F32),
             jax.ShapeDtypeStruct((reps // 2 - 1,) + gate_block, BF),
         ),
-        in_specs=[HBM, VMEM, VMEM, VMEM, HBM, HBM],
+        in_specs=[HBM, VMEM, VMEM, VMEM, HBM, HBM, HBM],
         out_specs=(VMEM, HBM, VMEM, VMEM, VMEM, VMEM, VMEM),
         scratch_shapes=scatter_scratch(half, width)
         + [
             pltpu.VMEM((2, half, width), BF),
             pltpu.VMEM((half, width), F32),
             pltpu.VMEM((reps // 2,) + down_block, BF),
-            pltpu.VMEM((reps // 2,) + down_block, BF),
+            pltpu.VMEM((reps - 1,) + down_block, BF),
+            pltpu.VMEM((reps // 2,) + gate_block, BF),
+            pltpu.VMEM((reps - 1,) + gate_block, BF),
             pltpu.VMEM((reps // 2,) + gate_block, BF),
             pltpu.VMEM((reps // 2,) + gate_block, BF),
         ]
-        + semaphores(4 * reps + SCATTER_COPIES + GATHER_COPIES, 4 * reps + 2),
+        + semaphores(
+            8 * (reps - 1) + 2 * reps + SCATTER_COPIES + GATHER_COPIES, 4 * reps + 2 * reps + 2
+        ),
         compiler_params=kernel_params(2),
         name="turn_back",
     )(
         parts.reshape(16, half, width), hidden, out_grad.reshape(2, half, width), gains,
-        down_p, gate_p,
+        down_p, gate_p, up_p,
     )
 
 
 def closing_kernel(
-    layout, attn_p, up_p, out_p, gate_sum, one_parts, two_parts, tokens, hidden_grad, gains, vectors,
+    layout, attn_p, out_q, gate_sum, up_sum, one_parts, two_parts, tokens, hidden_grad, gains, vectors,
     query_back, key_back, value_back, swish_back, gate_back, up_back, out_sum, branch_two,
     tokens_grad, vector_sum,
     even_1, cores_1, taken_1, even_2, cores_2, taken_2, sum_buf, rows_buf, vec_l, vec_y,
-    attn_l, attn_y, attn_s, up_l, up_y, up_s, out_l, out_y, send_sems, recv_sems, local_sems,
+    attn_l, attn_y, attn_s, out_l, out_y, send_sems, recv_sems, local_sems,
 ):
     links = Links(layout, send_sems, recv_sems, local_sems)
     device = links.device
@@ -872,19 +887,11 @@
             goal = pl.ds(pl.multiple_of(place * size, LANES), size)
             give(attn_s.at[place_at(mask), :, pl.ds(at, size)], target.at[:, goal], mask)
 
-    def up_return(mask):
-        give(up_s.at[place_at(mask)], up_back.at[place], mask)
-
     order = layout.team[::-1] + (0,)
-    items = []
-    for part, keep, taken, sums, give_back, paired in (
-        (attn_p, attn_l, attn_y, attn_s, attn_return, False),
-        (up_p, up_l, up_y, up_s, up_return, False),
-    ):
-        places = [place_at(m) for m in order]
-        plain = replica_items(layout, rep, part, keep, taken, places, sums, paired)
-        items += [with_return(item, m, give_back) for item, m in zip(plain, order)]
-    items += replica_items(layout, rep, out_p, out_l, out_y, range(4), out_sum)
+    items = replica_items(layout, rep, out_q, out_l, out_y, range(4), out_sum, True)
+    places = [place_at(m) for m in order]
+    plain = replica_items(layout, rep, attn_p, attn_l, attn_y, places, attn_s)
+    items += [with_return(item, m, attn_return) for item, m in zip(plain, order)]
     steps = scatter_stream(links, items, 2, 2)
 
     pieces = layout.pieces(width)
@@ -950,6 +957,7 @@
     def gate_return():
         for mask in layout.team + (0,):
             give(gate_sum.at[place_at(mask)], gate_back.at[place], mask)
+            give(up_sum.at[place_at(mask)], up_back.at[place], mask)
 
     one = scatter_steps_light(links, one_parts, even_1, cores_1, taken_1, finish_one)
     two = scatter_steps_light(links, two_parts, even_2, cores_2, taken_2, finish_two)
@@ -972,11 +980,11 @@
     links.finish()
 
 
-def closing_call(layout, attn_p, up_p, out_p, gate_sum, one_parts, two_parts, tokens, hidden_grad,
+def closing_call(layout, attn_p, out_q, gate_sum, up_sum, one_parts, two_parts, tokens, hidden_grad,
                  gains, vectors, back_widths):
     reps, shard = layout.reps, layout.shard
     half, width = hidden_grad.shape[1:]
-    attn_block, up_block, out_block = attn_p.shape[1:], up_p.shape[1:], out_p.shape[1:]
+    attn_block, up_block, out_block = attn_p.shape[1:], up_sum.shape, out_q.shape[1:]
     per = LANES // shard
     slots = layout.count // per
     stay = reps // 2
@@ -993,7 +1001,7 @@
             rows,
             jax.ShapeDtypeStruct((8, LANES), F32),
         ),
-        in_specs=[HBM, HBM, HBM, VMEM, HBM, HBM, VMEM, VMEM, VMEM, VMEM],
+        in_specs=[HBM, HBM, VMEM, VMEM, HBM, HBM, VMEM, VMEM, VMEM, VMEM],
         out_specs=(HBM,) * 6 + (VMEM,) * 4,
         scratch_shapes=scatter_scratch(half, width)
         + scatter_scratch(half, width)
@@ -1005,9 +1013,6 @@
             pltpu.VMEM((stay,) + attn_block, BF),
             pltpu.VMEM((reps - 1,) + attn_block, BF),
             pltpu.VMEM(attn_block, BF),
-            pltpu.VMEM((stay,) + up_block, BF),
-            pltpu.VMEM((reps - 1,) + up_block, BF),
-            pltpu.VMEM(up_block, BF),
             pltpu.VMEM((stay,) + out_block, BF),
             pltpu.VMEM((reps - 1,) + out_block, BF),
         ]
@@ -1015,7 +1020,7 @@
         compiler_params=kernel_params(3),
         name="closing",
     )(
-        attn_p, up_p, out_p, gate_sum, one_parts.reshape(16, half, width),
+        attn_p, out_q, gate_sum, up_sum, one_parts.reshape(16, half, width),
         two_parts.reshape(16, half, width), tokens.reshape(2, half, width), hidden_grad, gains, vectors,
     )
 
@@ -1129,6 +1134,14 @@
             low = layout.low(k)
             down_even.append(flip_rep(down_even[k & ~(1 << low)], low + 1))
 
+        def pair_sums(parts):
+            sums = []
+            for rel in range(0, reps, 2):
+                other = lax.dynamic_index_in_dim(parts, rep ^ (rel + 1), 0, keepdims=False)
+                own = lax.dynamic_index_in_dim(parts, rep ^ rel, 0, keepdims=False)
+                sums.append((own.astype(F32) + flip_rep(other, 0).astype(F32)).astype(BF))
+            return jnp.stack(sums)
+
         def finish_pairs(first, rest):
             sums = [first] + [rest[k] for k in range(reps // 2 - 1)]
             for k in range(reps // 2 - 1, 0, -1):
@@ -1221,15 +1234,17 @@
         gate_parts = dot_tn(normed_two, gate_low).astype(BF)
         up_parts = dot_tn(normed_two, up_low).astype(BF)
         normed_parts = (dot_nt(gate_low, gate_w) + dot_nt(up_low, up_w)).astype(BF)
-        hidden_grad, branch_one_grad, vectors, down_first, down_rest, gate_first, gate_rest = turn_back_call(
+        hidden_grad, branch_one_grad, vectors, mlp_down_grad, gate_sum, up_first, up_rest = turn_back_call(
             layout, normed_parts, hidden, out_grad_low, gains_two,
             down_parts.reshape(reps, 4, -1, width), gate_parts.reshape(reps, 8, shard, -1),
+            up_parts.reshape(reps, 8, shard, -1),
         )
         branch_one_grad = branch_one_grad.reshape(group_rows, width)
-        gate_sum = finish_pairs(gate_first, gate_rest).astype(BF)
-        mlp_down_grad = finish_pairs(down_first, down_rest)
+        up_sum = finish_pairs(up_first, up_rest).astype(BF)
 
         mixed_grad = dot_nt(branch_one_grad, out_w)
+        out_parts = dot_tn(mixed, branch_one_grad).astype(BF)
+        out_pairs = pair_sums(out_parts.reshape(reps, 4, -1, width))
         _, pull_mix = jax.vjp(mix, gate_raw, retained)
         gate_grad, retained_grad = pull_mix(mixed_grad)
         gate_grad = gate_grad.astype(BF)
@@ -1246,15 +1261,12 @@
         key_grad = rotate_back(key_turn_grad.reshape(group_rows, key_size), key_factor).astype(BF)
         attn_grads = jnp.concatenate([query_grad, key_grad, value_grad, gate_grad], axis=1)
         attn_parts = dot_tn(normed_one, attn_grads).astype(BF)
-        out_parts = dot_tn(mixed, branch_one_grad).astype(BF)
         one_parts = dot_nt(attn_grads, attn_w).astype(BF)
         q_back, k_back, v_back, g_back, gate_back, up_back, out_sum, branch_two, tokens_grad, vectors = (
             closing_call(
                 layout,
                 attn_parts.reshape(reps, 8, shard, -1),
-                up_parts.reshape(reps, 8, shard, -1),
-                out_parts.reshape(reps, 4, -1, width),
-                gate_sum, one_parts, two_parts, tokens, hidden_grad, gains_one, vectors,
+                out_pairs, gate_sum, up_sum, one_parts, two_parts, tokens, hidden_grad, gains_one, vectors,
                 [w.shape[1] for w in (query_weight, key_weight, value_weight, gate_weight)],
             )
         )

time: 607 us -> 614 us (1.012)
  waiting for transfers between devices: 26 us -> 18.2 us
  matrix products: 81 us -> 88.2 us
    pallas_call x1, Pallas kernels: 60 us -> 84.3 us  [turn_back_call(): pl.pallas_call(functools.partial(turn_back_kernel, layout), out_shape=(ja...]
    pallas_call x1, Pallas kernels: 153 us -> 131 us  [closing_call(): pl.pallas_call(functools.partial(closing_kernel, layout), out_shape=tuple...]
    ppermute x3 -> x4, waiting for transfers between devices: 26 us -> 18.1 us  [flip_rep(): return lax.ppermute(values, 'dp', [(d, d ^ mask) for d in range(count)])]
    dot_general x5, matrix products: 24.1 us -> 31.3 us  [dot_tn(): lax.dot_general(left, right, (((0,), (0,)), ((), ())), preferred_element_...]
  transfers between devices with their start and end apart: 5 -> 6, of which waited for: 1 -> 1; matrix products, arithmetic and copies ran while one was open for 10% -> 12% of each run, Pallas kernels for 26% -> 0%
where the time goes in v1:
time: 614 us; the launch traced here: 605 us
  Pallas kernels  427 us (70%)
  matrix products  88.2 us (14%)
  local copies, waits for them, and re-layouts  30.7 us (5%)
  other arithmetic  28.9 us (5%)
  waiting for transfers between devices  18.2 us (3%)
  starting transfers between devices  10 us (2%)
    pallas_call x1, Pallas kernels, opening_call(): pl.pallas_call(functools.partial(opening_kernel, layout), out_shape=(jax....  134 us
    pallas_call x1, Pallas kernels, closing_call(): pl.pallas_call(functools.partial(closing_kernel, layout), out_shape=tuple...  131 us
    pallas_call x1, Pallas kernels, turn_back_call(): pl.pallas_call(functools.partial(turn_back_kernel, layout), out_shape=(ja...  84.3 us
    pallas_call x1, Pallas kernels, turn_call(): pl.pallas_call(functools.partial(turn_kernel, layout), out_shape=(jax.Sha...  77.3 us
    dot_general x5, matrix products, dot_tn(): lax.dot_general(left, right, (((0,), (0,)), ((), ())), preferred_element_...  31.3 us
    dot_general x5, matrix products, dot(): return jnp.dot(left, right, preferred_element_type=F32)  26.6 us
    dot_general x5, matrix products, dot_nt(): lax.dot_general(left, right, (((1,), (1,)), ((), ())), preferred_element_...  25.4 us
    ppermute x4, waiting for transfers between devices, flip_rep(): return lax.ppermute(values, 'dp', [(d, d ^ mask) for d in range(count)])  18.1 us
  transfers between devices with their start and end apart: 6, of which 1 were waited for; matrix products, arithmetic and copies ran while one was open for 12% of the time, Pallas kernels for 0%

profile of v1, /device:TPU:0, one launch (start us, length us, event | category | flops | bytes accessed | tf_op | source)
XLA Modules:
  0.0 604.6 jit_solution(6699293130386017950)
XLA Ops:
  0.7 1.8 collective-permute-start
  2.5 0.7 tile.40
  5.5 0.9 fusion.32
  7.0 1.4 reshape.798
  8.8 1.0 reshape.799.gate_src
  10.6 1.0 reshape.801.up_src
  12.9 0.9 multiply_convert_fusion.3
  13.9 0.8 copy-done.27
  14.7 134.4 %opening.1 = (bf16[32,8,128]{2,1,0:T(8,128)(2,1)}, bf16[16,64,2048]{2,1,0:T(8,128)(2,1)}, bf16[16,64,2048]{2,1,0:T(8,128)(2,1)}, bf16[4,8,64,1536]{3,2,1,0:T(8,1...) custom-call(bf16[1,8,128]{2,1,0:T(8,128)(2,1)} %bitcast.191, ...), custom_call_target="tpu_custom_call" | custom-call | tf_op jit(solution)/shard_map/opening/pallas_call | solution.py:618
  149.1 0.9 slice_convert_fusion.1
  151.2 0.9 convert_reduce_fusion
  152.3 1.9 multiply_sine_fusion
  154.2 1.4 power_multiply_fusion
  155.7 10.3 %fusion.34 = f32[1024,1536]{1,0:T(8,128)S(1)} fusion(bf16[1024,2048]{1,0:T(8,128)(2,1)} %bitcast.196, bf16[2048,1536]{1,0:T(8,128)(2,1)} %bitcast.192), kind=kOutput, calls=%fused_computation.133 | convolution fusion | flops 6442450944 | bytes 16777216 | tf_op jit(solution)/shard_map/dot_general | solution.py:1046
  166.6 2.0 copy-done
  168.6 1.6 fusion.11
  171.5 2.6 multiply_convert_fusion.2
  174.2 0.7 pad.12.gains
  175.5 4.4 convolution_convert_fusion.3
  179.9 2.3 pad_maximum_fusion.down_in
  182.2 77.3 %turn.1 = (f32[2,64,2048]{2,1,0:T(8,128)}, bf16[16,64,2048]{2,1,0:T(8,128)(2,1)}, bf16[4,8,64,512]{3,2,1,0:T(8,128)(2,1)}, bf16[4,8,64,512]{3,2,1,0:T(8,128)(2,1)}, bf16[4,128,2048]{2,1,0:T(8,128)(2,1)}) custom-call(bf16[16,64,2048]{2,1,0:T(8,128)(2,1)} %bitcast.161, bf16[2,64,2048]{2,1,0:T(8,128)(2,1)} %bitcast.158, f32[8,2048]{1,0:T(8,128)} %pad.12.gains, ...), custom_call_target="tpu_custom_call" | custom-call | tf_op jit(solution)/shard_map/turn/pallas_call | solution.py:706
  259.5 5.3 fusion.36
  264.9 2.3 fusion.35
  267.7 3.8 multiply_convert_fusion
  271.6 3.8 convolution_convert_fusion.6
  275.4 2.4 fusion.37
  277.8 12.5 %convolution_convert_fusion.5 = bf16[2048,512]{1,0:T(8,128)(2,1)} fusion(bf16[1024,2048]{1,0:T(8,128)(2,1)S(1)} %bitcast.205, bf16[1024,512]{1,0:T(8,128)(2,1)S(1)} %get-tuple-element.95), kind=kOutput, calls=%fused_computation.11 | convolution fusion | flops 2148532224 | bytes 7340032 | tf_op jit(solution)/shard_map/dot_general | solution.py:1054
  290.2 3.8 convolution_convert_fusion.7
  294.1 4.4 add_convert_fusion
  298.5 84.3 %turn_back.1 = (f32[2,64,2048]{2,1,0:T(8,128)}, bf16[16,64,2048]{2,1,0:T(8,128)(2,1)}, f32[8,2048]{1,0:T(8,128)}, f32[4,32,2048]{2,1,0:T(8,128)}, bf16[8,64,512]...) custom-call(bf16[16,64,2048]{2,1,0:T(8,128)(2,1)} %bitcast.160, ...), custom_call_target="tpu_custom_call" | custom-call | tf_op jit(solution)/shard_map/turn_back/pallas_call | solution.py:812
  382.8 6.3 %multiply_reduce_fusion = (f32[1024]{0:T(1024)S(1)}, f32[1024,512]{1,0:T(8,128)S(1)}) fusion(f32[16,64,512]{2,1,0:T(8,128)S(1)} %get-tuple-element.117, f32[1024]{0:T(1024)S(1)} %div.123, f32[1024,1536]{1,0:T(8,128)} %copy-done, bf16[1024,2048]{1,0:T(8,128)(2,1)} %bitcast.200, bf16[512,2048]{1,0:T(8,128)(2,1)} %bitcast.206), kind=kOutput, calls=%fused_computation.27 | convolution fusion | flops 2151676928 | bytes 12591104 | tf_op jit(solution)/shard_map/dot_general | solution.py:1050
  389.1 3.2 fusion.31
  392.5 0.7 copy-done.21
  393.8 1.7 fusion.12
  396.2 0.7 copy-done.9
  396.9 2.4 convolution_convert_fusion.4
  399.7 0.8 copy-done.2
  401.3 1.8 collective-permute-start.3
  403.3 2.0 copy-done.30
  405.4 8.8 %convolution_convert_fusion = bf16[2048,1536]{1,0:T(8,128)(2,1)} fusion(bf16[1024,2048]{1,0:T(8,128)(2,1)S(1)} %bitcast.197, bf16[1024,1536]{1,0:T(8,128)(2,1)S(1)} %constant_dynamic-update-slice_fusion), kind=kOutput, calls=%fused_computation.2 | convolution fusion | flops 6445596672 | bytes 13631488 | tf_op jit(solution)/shard_map/dot_general | solution.py:1054
  414.2 8.5 %convolution_convert_fusion.1 = bf16[1024,2048]{1,0:T(8,128)(2,1)} fusion(bf16[1024,1536]{1,0:T(8,128)(2,1)S(1)} %constant_dynamic-update-slice_fusion, bf16[2048,1536]{1,0:T(8,128)(2,1)S(1)} %bitcast.195), kind=kOutput, calls=%fused_computation.3 | convolution fusion | flops 6444548096 | bytes 13631488 | tf_op jit(solution)/shard_map/dot_general | solution.py:1050
  422.8 0.7 collective-permute-start.4
  423.5 4.3 convolution_convert_fusion.2
  428.2 1.1 pad_maximum_fusion.1.out_q
  429.2 18.1 %collective-permute-done.4 = bf16[8,64,512]{2,1,0:T(8,128)(2,1)S(1)} collective-permute-done((bf16[8,64,512]{2,1,0:T(8,128)(2,1)S(1)}, bf16[8,64,512]{2,1,0:T(8,128)(2,1)S(1)}, u32[]{:S(2)}, u32[]{:S(2)}) %collective-permute-start.4) | collective-permute-done | bytes 524320 | tf_op jit(solution)/shard_map/ppermute | solution.py:1130
  447.4 1.0 add_convert_fusion.2.up_sum
  448.3 130.7 %closing.1 = (bf16[64,2048]{1,0:T(8,128)(2,1)}, bf16[64,2048]{1,0:T(8,128)(2,1)}, bf16[64,4096]{1,0:T(8,128)(2,1)}, bf16[64,4096]{1,0:T(8,128)(2,1)}, bf16[8,64,...) custom-call(bf16[4,8,64,1536]{3,2,1,0:T(8,128)(2,1)} %bitcast.154, ...), custom_call_target="tpu_custom_call" | custom-call | tf_op jit(solution)/shard_map/closing/pallas_call | solution.py:993
  579.0 2.1 convert_element_type.219
  581.1 5.4 collective-permute-start.5
  586.5 0.7 constant_dynamic-slice_fusion
  587.8 1.7 reshape.850
  589.5 0.7 copy.53
  590.1 1.4 reshape.844
  592.2 0.7 copy.54
  592.9 1.4 reshape.846
  594.5 0.9 copy-done.23
  595.3 1.0 convert_element_type.217
  596.4 1.0 convert_element_type.218
  597.4 0.8 convert_element_type.215
  598.2 0.8 convert_element_type.216
  599.1 0.9 fusion.15
  600.0 2.2 convert_element_type.221
  602.2 1.0 copy.68
  603.2 1.0 copy.69
  (159 shorter events, 14.4 us)
Async XLA Ops:
  0.6 9.2 %copy-start.25 = (bf16[64,4096]{1,0:T(8,128)(2,1)S(1)}, bf16[64,4096]{1,0:T(8,128)(2,1)}, u32[]{:S(2)}) copy-start(bf16[64,4096]{1,0:T(8,128)(2,1)} %param.27) | copy-start | bytes 1572868
  0.7 13.2 %collective-permute-start = (bf16[128,2048]{1,0:T(8,128)(2,1)}, bf16[128,2048]{1,0:T(8,128)(2,1)S(1)}, u32[]{:S(2)}, u32[]{:S(2)}) collective-permute-start(bf16[128,2048]{1,0:T(8,128)(2,1)} %param.23), channel_id=1, source_target_pairs={{0,0},{1,4},{2,16},{3,20},{4,1},{5,5},{6,17},{7,21},{8,2},{9,6},{1... | collective-permute-start | bytes 1572872 | tf_op jit(solution)/shard_map/ppermute | solution.py:1117
  8.8 4.1 copy-start.26
  13.9 0.8 copy-start.27
  152.0 27.9 %collective-permute-start.1 = (bf16[128,2048]{1,0:T(8,128)(2,1)}, bf16[128,2048]{1,0:T(8,128)(2,1)}, u32[]{:S(2)}, u32[]{:S(2)}) collective-permute-start(bf16[128,2048]{1,0:T(8,128)(2,1)} %param.28), channel_id=1, source_target_pairs={{0,16},{1,17},{2,18},{3,19},{4,20},{5,21},{6,22},{7,23},{8,24},{9,... | collective-permute-start | bytes 1572872 | tf_op jit(solution)/shard_map/ppermute | solution.py:1130
  155.6 10.5 %copy-start.1 = (f32[1024,128]{1,0:T(8,128)}, f32[1024,128]{1,0:T(8,128)S(1)}, u32[]{:S(2)}) copy-start(f32[1024,128]{1,0:T(8,128)S(1)} %get-tuple-element.54) | copy-start | bytes 1572868
  155.6 10.5 %copy-start.3 = (f32[1024,128]{1,0:T(8,128)}, f32[1024,128]{1,0:T(8,128)S(1)}, u32[]{:S(2)}) copy-start(f32[1024,128]{1,0:T(8,128)S(1)} %get-tuple-element.53) | copy-start | bytes 1572868
  166.0 2.6 copy-start
  166.1 4.1 copy-start.6
  168.6 1.6 copy-start.11
  168.6 1.6 copy-start.13
  168.6 1.6 copy-start.15
  170.2 0.7 copy-start.20
  171.5 4.0 copy-start.34
  174.2 5.7 copy-start.8
  259.5 5.4 copy-start.33
  259.5 5.4 copy-start.37
  264.9 2.3 copy-start.31
  264.9 2.9 copy-start.35
  271.6 18.7 %copy-start.40 = (bf16[1024,512]{1,0:T(8,128)(2,1)}, bf16[1024,512]{1,0:T(8,128)(2,1)S(1)}, u32[]{:S(2)}) copy-start(bf16[1024,512]{1,0:T(8,128)(2,1)S(1)} %get-tuple-element.93) | copy-start | bytes 3145732
  271.6 3.8 copy-start.38
  392.3 1.0 copy-start.21
  392.3 1.4 copy-start.7
  393.7 1.8 copy-start.14
  393.7 1.8 copy-start.16
  393.8 2.1 copy-start.12
  393.8 2.4 copy-start.32
  395.5 1.4 copy-start.9
  396.9 2.4 copy-start.4
  399.5 1.0 copy-start.2
  401.1 26.7 %collective-permute-start.2 = (bf16[4,32,2048]{2,1,0:T(8,128)(2,1)S(1)}, bf16[4,32,2048]{2,1,0:T(8,128)(2,1)S(1)}, u32[]{:S(2)}, u32[]{:S(2)}) collective-permute-start(bf16[4,32,2048]{2,1,0:T(8,128)(2,1)S(1)} %get-tuple-element.98), channel_id=1, source_target_pairs={{0,4},{1,5},{2,6},{3,7},{4,0},{5,1},{6,2},{7,3},{8,12},{9,13},{10,... | collective-permute-start | bytes 1572872 | tf_op jit(solution)/shard_map/ppermute | solution.py:1130
  401.3 26.4 %collective-permute-start.3 = (bf16[4,32,2048]{2,1,0:T(8,128)(2,1)S(1)}, bf16[4,32,2048]{2,1,0:T(8,128)(2,1)S(1)}, u32[]{:S(2)}, u32[]{:S(2)}) collective-permute-start(bf16[4,32,2048]{2,1,0:T(8,128)(2,1)S(1)} %get-tuple-element.99), channel_id=1, source_target_pairs={{0,4},{1,5},{2,6},{3,7},{4,0},{5,1},{6,2},{7,3},{8,12},{9,13},{10,... | collective-permute-start | bytes 1572872 | tf_op jit(solution)/shard_map/ppermute | solution.py:1130
  403.2 2.2 copy-start.30
  403.2 11.0 %slice-start = ((s8[6291456]{0:T(1024)(128)(4,1)}), s8[4194304]{0:T(1024)(128)(4,1)S(1)}, s32[]{:S(2)}) async-start(s8[6291456]{0:T(1024)(128)(4,1)} %bitcast.193), calls=%async_computation | async-start | bytes 8388608
  405.4 8.8 %slice-start.1 = ((s8[6291456]{0:T(1024)(128)(4,1)}), s8[2097152]{0:T(1024)(128)(4,1)S(1)}, s32[]{:S(2)}) async-start(s8[6291456]{0:T(1024)(128)(4,1)} %bitcast.193), calls=%async_computation.1 | async-start | bytes 4194304
  414.2 8.6 %copy-start.39 = (bf16[1,8,64,512]{3,2,1,0:T(8,128)(2,1)S(1)}, bf16[1,8,64,512]{3,2,1,0:T(8,128)(2,1)}, u32[]{:S(2)}) copy-start(bf16[1,8,64,512]{3,2,1,0:T(8,128)(2,1)} %get-tuple-element.68) | copy-start | bytes 1572868
  414.2 9.2 %copy-start.36 = (bf16[4,128,2048]{2,1,0:T(8,128)(2,1)S(1)}, bf16[4,128,2048]{2,1,0:T(8,128)(2,1)}, u32[]{:S(2)}) copy-start(bf16[4,128,2048]{2,1,0:T(8,128)(2,1)} %get-tuple-element.61) | copy-start | bytes 6291460
  414.2 9.2 %copy-start.41 = (bf16[1024,512]{1,0:T(8,128)(2,1)S(1)}, bf16[1024,512]{1,0:T(8,128)(2,1)}, u32[]{:S(2)}) copy-start(bf16[1024,512]{1,0:T(8,128)(2,1)} %copy-done.40) | copy-start | bytes 3145732
  422.8 24.6 %collective-permute-start.4 = (bf16[8,64,512]{2,1,0:T(8,128)(2,1)S(1)}, bf16[8,64,512]{2,1,0:T(8,128)(2,1)S(1)}, u32[]{:S(2)}, u32[]{:S(2)}) collective-permute-start(bf16[8,64,512]{2,1,0:T(8,128)(2,1)S(1)} %bitcast.214), channel_id=1, source_target_pairs={{0,16},{1,17},{2,18},{3,19},{4,20},{5,21},{6,22},{7,23},{8,24},{9,... | collective-permute-start | bytes 1572872 | tf_op jit(solution)/shard_map/ppermute | solution.py:1130
  427.7 19.6 %copy-start.18 = (f32[8,64,512]{2,1,0:T(8,128)S(1)}, f32[8,64,512]{2,1,0:T(8,128)}, u32[]{:S(2)}) copy-start(f32[8,64,512]{2,1,0:T(8,128)} %get-tuple-element.67) | copy-start | bytes 3145732
  581.1 18.9 %collective-permute-start.5 = (bf16[128,2048]{1,0:T(8,128)(2,1)}, bf16[128,2048]{1,0:T(8,128)(2,1)}, u32[]{:S(2)}, u32[]{:S(2)}) collective-permute-start(bf16[128,2048]{1,0:T(8,128)(2,1)} %bitcast.71), channel_id=1, source_target_pairs={{0,0},{4,1},{16,2},{20,3},{1,4},{5,5},{17,6},{21,7},{2,8},{6,9},{1... | collective-permute-start | bytes 1572872 | tf_op jit(solution)/shard_map/ppermute | solution.py:1274
  589.4 2.1 copy-start.24
  592.2 2.1 copy-start.5
  592.9 1.4 copy-start.10
  594.3 1.0 copy-start.23
  594.3 2.1 copy-start.22
  594.4 3.0 copy-start.29
  594.4 3.8 copy-start.28
  598.2 4.0 copy-start.19
  600.0 3.2 copy-start.17

commit v2 on v1

--- a/solution.py
+++ b/solution.py
@@ -50,6 +50,12 @@
             total += ((rep >> i) & 1) << b
         return total
 
+    def head_part(self, rep):
+        return (rep % (self.reps // 2)) * 2 + rep // (self.reps // 2)
+
+    def head_rep(self, part):
+        return (part % 2) * (self.reps // 2) + part // 2
+
     def low(self, rel):
         return (rel & -rel).bit_length() - 1 if rel else len(self.rep_bits)
 
@@ -546,13 +552,16 @@
         return (
             lambda: None,
             own.at[part],
-            lambda rel: target.at[xor_index(rel, rep, layout.reps), part],
-        )
-
-    items = [attn_item(0)] + [row_item(out_own, out_w, part) for part in range(4)]
+            lambda rel: target(xor_index(rel, rep, layout.reps)).at[part],
+        )
+
+    def out_slot(owner):
+        return out_w.at[layout.head_part(owner)]
+
+    items = [attn_item(0)] + [row_item(out_own, out_slot, part) for part in range(4)]
     items += [attn_item(mask) for mask in layout.team]
     out_load.wait()
-    keeps.append(links.local(out_own, out_w.at[rep]))
+    keeps.append(links.local(out_own, out_slot(rep)))
     steps, stream_end = gather_stream(links, items, 3)
     steps[0]()
     for b in range(1, layout.bits):
@@ -726,7 +735,7 @@
 
 
 def turn_back_kernel(
-    layout, parts, hidden, out_grad, gains, down_p, gate_p, up_p,
+    layout, parts, hidden, out_grad, gains, down_p, hidden_p,
     hidden_grad, all_rows, vectors, down_sum, gate_sum, up_first, up_rest,
     even, cores, taken, low_buf, sum_buf, down_l, down_y, gate_l, gate_y, up_l, up_y,
     send_sems, recv_sems, local_sems,
@@ -736,6 +745,8 @@
     _, half, width = hidden.shape
     links.greet((CORE, NEAR, layout.far) + tuple(1 << b for b in layout.rep_bits))
 
+    columns = gate_sum.shape[2]
+
     def item(part, keep, taken, at, first, rest):
         def finish(k, value):
             if k:
@@ -744,7 +755,7 @@
                 first[at] = value.astype(first.dtype)
 
         return (
-            lambda rel: part.at[xor_index(rel, rep, layout.reps), at],
+            lambda rel: part.at[xor_index(rel, rep, layout.reps), at, :, pl.ds(columns, columns)],
             lambda k: keep.at[k, at],
             lambda k: taken.at[k, at],
             finish,
@@ -752,9 +763,12 @@
 
     pairs = [pl.ds(2 * part, 2) for part in range(4)]
     items = replica_items(layout, rep, down_p, down_l, down_y, range(4), down_sum)
-    items += replica_items(layout, rep, gate_p, gate_l, gate_y, pairs, gate_sum)
+    gates = replica_items(layout, rep, hidden_p, gate_l, gate_y, pairs, gate_sum)
+    items += [
+        ((lambda rel, part=g[0]: part(rel).at[:, :, pl.ds(0, columns)]),) + g[1:] for g in gates
+    ]
     steps = scatter_stream(links, items, 2, 2)
-    late = pair_stream(links, [item(up_p, up_l, up_y, at, up_first, up_rest) for at in pairs], 2)
+    late = pair_stream(links, [item(hidden_p, up_l, up_y, at, up_first, up_rest) for at in pairs], 2)
     for k, more in enumerate(late):
         steps[min(k + 5, 11)] = both(steps[min(k + 5, 11)], more)
     pieces = layout.pieces(width)
@@ -805,10 +819,11 @@
     return [item(at) for at in places]
 
 
-def turn_back_call(layout, parts, hidden, out_grad, gains, down_p, gate_p, up_p):
+def turn_back_call(layout, parts, hidden, out_grad, gains, down_p, hidden_p):
     half, width = hidden.shape[1:]
     reps = layout.reps
-    down_block, gate_block = down_p.shape[1:], gate_p.shape[1:]
+    down_block = down_p.shape[1:]
+    gate_block = hidden_p.shape[1:3] + (hidden_p.shape[3] // 2,)
     return pl.pallas_call(
         functools.partial(turn_back_kernel, layout),
         out_shape=(
@@ -820,7 +835,7 @@
             jax.ShapeDtypeStruct(gate_block, F32),
             jax.ShapeDtypeStruct((reps // 2 - 1,) + gate_block, BF),
         ),
-        in_specs=[HBM, VMEM, VMEM, VMEM, HBM, HBM, HBM],
+        in_specs=[HBM, VMEM, VMEM, VMEM, HBM, HBM],
         out_specs=(VMEM, HBM, VMEM, VMEM, VMEM, VMEM, VMEM),
         scratch_shapes=scatter_scratch(half, width)
         + [
@@ -840,7 +855,7 @@
         name="turn_back",
     )(
         parts.reshape(16, half, width), hidden, out_grad.reshape(2, half, width), gains,
-        down_p, gate_p, up_p,
+        down_p, hidden_p,
     )
 
 
@@ -1085,7 +1100,7 @@
         hidden_size = mlp_gate.shape[1]
         ff_block = hidden_size // count
         group_rows = 8 * local_rows
-        home = [layout.device(d % reps, d // reps) for d in range(count)]
+        home = [layout.device(layout.head_rep(d % reps), d // reps) for d in range(count)]
         head_perm = [(d, home[d]) for d in range(count)]
         head_back = [(b, a) for a, b in head_perm]
 
@@ -1137,8 +1152,10 @@
         def pair_sums(parts):
             sums = []
             for rel in range(0, reps, 2):
-                other = lax.dynamic_index_in_dim(parts, rep ^ (rel + 1), 0, keepdims=False)
-                own = lax.dynamic_index_in_dim(parts, rep ^ rel, 0, keepdims=False)
+                other = lax.dynamic_index_in_dim(
+                    parts, layout.head_part(rep ^ (rel + 1)), 0, keepdims=False
+                )
+                own = lax.dynamic_index_in_dim(parts, layout.head_part(rep ^ rel), 0, keepdims=False)
                 sums.append((own.astype(F32) + flip_rep(other, 0).astype(F32)).astype(BF))
             return jnp.stack(sums)
 
@@ -1231,13 +1248,11 @@
         gate_low, up_low = (g.astype(BF) for g in pull_act(dot_nt(cot_all, down_w)))
         two_parts = dot(product, down_w).astype(BF)
         down_parts = dot_tn(product, cot_all).astype(BF)
-        gate_parts = dot_tn(normed_two, gate_low).astype(BF)
-        up_parts = dot_tn(normed_two, up_low).astype(BF)
+        hidden_parts = dot_tn(normed_two, jnp.concatenate([gate_low, up_low], axis=1)).astype(BF)
         normed_parts = (dot_nt(gate_low, gate_w) + dot_nt(up_low, up_w)).astype(BF)
         hidden_grad, branch_one_grad, vectors, mlp_down_grad, gate_sum, up_first, up_rest = turn_back_call(
             layout, normed_parts, hidden, out_grad_low, gains_two,
-            down_parts.reshape(reps, 4, -1, width), gate_parts.reshape(reps, 8, shard, -1),
-            up_parts.reshape(reps, 8, shard, -1),
+            down_parts.reshape(reps, 4, -1, width), hidden_parts.reshape(reps, 8, shard, -1),
         )
         branch_one_grad = branch_one_grad.reshape(group_rows, width)
         up_sum = finish_pairs(up_first, up_rest).astype(BF)

time: 614 us -> 600 us (0.977)
  the two profiles are of different devices: /device:TPU:0 before, /device:TPU:2 now
where the time goes in v2:
time: 600 us; the launch traced here: 590 us
  Pallas kernels  413 us (69%)
  matrix products  78.2 us (13%)
  local copies, waits for them, and re-layouts  30.8 us (5%)
  waiting for transfers between devices  29.4 us (5%)
  other arithmetic  28.7 us (5%)
  starting transfers between devices  8.65 us (1%)
    pallas_call x1, Pallas kernels, closing_call(): pl.pallas_call(functools.partial(closing_kernel, layout), out_shape=tuple...  131 us
    pallas_call x1, Pallas kernels, opening_call(): pl.pallas_call(functools.partial(opening_kernel, layout), out_shape=(jax....  122 us
    pallas_call x1, Pallas kernels, turn_back_call(): pl.pallas_call(functools.partial(turn_back_kernel, layout), out_shape=(ja...  85 us
    pallas_call x1, Pallas kernels, turn_call(): pl.pallas_call(functools.partial(turn_kernel, layout), out_shape=(jax.Sha...  75.1 us
    dot_general x5, matrix products, dot(): return jnp.dot(left, right, preferred_element_type=F32)  26.6 us
    dot_general x5, matrix products, dot_nt(): lax.dot_general(left, right, (((1,), (1,)), ((), ())), preferred_element_...  25.4 us
    dot_general x4, matrix products, dot_tn(): lax.dot_general(left, right, (((0,), (0,)), ((), ())), preferred_element_...  21.2 us
    ppermute x4, waiting for transfers between devices, flip_rep(): return lax.ppermute(values, 'dp', [(d, d ^ mask) for d in range(count)])  17.7 us
  transfers between devices with their start and end apart: 6, of which 2 were waited for; matrix products, arithmetic and copies ran while one was open for 12% of the time, Pallas kernels for 0%

profile of v2, /device:TPU:2, one launch (start us, length us, event | category | flops | bytes accessed | tf_op | source)
XLA Modules:
  0.0 590.5 jit_solution(15779373758174925294)
XLA Ops:
  0.7 3.5 collective-permute-start
  4.3 0.7 tile.40
  7.3 0.9 fusion.36
  8.9 1.4 reshape.795
  10.7 1.0 reshape.796.gate_src
  12.5 1.0 reshape.798.up_src
  14.8 0.9 multiply_convert_fusion.3
  15.8 0.8 copy-done.27
  16.6 121.9 %opening.1 = (bf16[32,8,128]{2,1,0:T(8,128)(2,1)}, bf16[16,64,2048]{2,1,0:T(8,128)(2,1)}, bf16[16,64,2048]{2,1,0:T(8,128)(2,1)}, bf16[4,8,64,1536]{3,2,1,0:T(8,1...) custom-call(bf16[1,8,128]{2,1,0:T(8,128)(2,1)} %bitcast.186, ...), custom_call_target="tpu_custom_call" | custom-call | tf_op jit(solution)/shard_map/opening/pallas_call | solution.py:627
  138.4 0.9 slice_convert_fusion.1
  140.5 0.9 convert_reduce_fusion
  141.7 1.9 multiply_sine_fusion
  143.5 1.4 power_multiply_fusion
  145.0 10.3 %fusion.38 = f32[1024,1536]{1,0:T(8,128)S(1)} fusion(bf16[1024,2048]{1,0:T(8,128)(2,1)} %bitcast.191, bf16[2048,1536]{1,0:T(8,128)(2,1)} %bitcast.187), kind=kOutput, calls=%fused_computation.136 | convolution fusion | flops 6442450944 | bytes 16777216 | tf_op jit(solution)/shard_map/dot_general | solution.py:1061
  155.9 2.1 copy-done
  158.0 1.7 fusion.14
  161.0 2.6 multiply_convert_fusion.2
  163.6 0.7 pad.12.gains
  165.0 4.4 convolution_convert_fusion.3
  169.3 2.3 pad_maximum_fusion.down_in
  171.6 75.1 %turn.1 = (f32[2,64,2048]{2,1,0:T(8,128)}, bf16[16,64,2048]{2,1,0:T(8,128)(2,1)}, bf16[4,8,64,512]{3,2,1,0:T(8,128)(2,1)}, bf16[4,8,64,512]{3,2,1,0:T(8,128)(2,1)}, bf16[4,128,2048]{2,1,0:T(8,128)(2,1)}) custom-call(bf16[16,64,2048]{2,1,0:T(8,128)(2,1)} %bitcast.158, bf16[2,64,2048]{2,1,0:T(8,128)(2,1)} %bitcast.154, f32[8,2048]{1,0:T(8,128)} %pad.12.gains, ...), custom_call_target="tpu_custom_call" | custom-call | tf_op jit(solution)/shard_map/turn/pallas_call | solution.py:715
  246.8 5.3 fusion.40
  252.1 2.3 fusion.39
  255.0 3.8 multiply_convert_fusion
  258.8 2.4 fusion.41
  261.2 6.4 %convolution_convert_fusion.4 = bf16[2048,1024]{1,0:T(8,128)(2,1)} fusion(bf16[1024,2048]{1,0:T(8,128)(2,1)S(1)} %bitcast.199, bf16[1024,512]{1,0:T(8,128)(2,1)S(1)} %get-tuple-element.95, bf16[1024,512]{1,0:T(8,128)(2,1)S(1)} %get-tuple-element.94), kind=kOutput, calls=%fused_computation.6 | convolution fusion | flops 4301258752 | bytes 10485760 | tf_op jit(solution)/shard_map/dot_general | solution.py:1069
  267.6 3.7 convolution_convert_fusion.6
  271.3 4.4 add_convert_fusion
  275.7 85.0 %turn_back.1 = (f32[2,64,2048]{2,1,0:T(8,128)}, bf16[16,64,2048]{2,1,0:T(8,128)(2,1)}, f32[8,2048]{1,0:T(8,128)}, f32[4,32,2048]{2,1,0:T(8,128)}, bf16[8,64,512]...) custom-call(bf16[16,64,2048]{2,1,0:T(8,128)(2,1)} %bitcast.157, ...), custom_call_target="tpu_custom_call" | custom-call | tf_op jit(solution)/shard_map/turn_back/pallas_call | solution.py:827
  360.7 6.3 %multiply_reduce_fusion = (f32[1024]{0:T(1024)S(1)}, f32[1024,512]{1,0:T(8,128)S(1)}) fusion(f32[16,64,512]{2,1,0:T(8,128)S(1)} %get-tuple-element.117, f32[1024]{0:T(1024)S(1)} %div.151, f32[1024,1536]{1,0:T(8,128)} %copy-done, bf16[1024,2048]{1,0:T(8,128)(2,1)} %bitcast.195, bf16[512,2048]{1,0:T(8,128)(2,1)} %bitcast.200), kind=kOutput, calls=%fused_computation.29 | convolution fusion | flops 2151676928 | bytes 12591104 | tf_op jit(solution)/shard_map/dot_general | solution.py:1065
  367.0 3.1 fusion.35
  370.4 0.7 copy-done.21
  371.7 1.7 fusion.15
  374.1 0.7 copy-done.9
  374.8 2.4 convolution_convert_fusion.5
  377.7 0.8 copy-done.2
  379.2 1.9 collective-permute-start.3
  381.3 2.0 copy-done.30
  383.4 8.7 %convolution_convert_fusion = bf16[2048,1536]{1,0:T(8,128)(2,1)} fusion(bf16[1024,2048]{1,0:T(8,128)(2,1)S(1)} %bitcast.192, bf16[1024,1536]{1,0:T(8,128)(2,1)S(1)} %constant_dynamic-update-slice_fusion), kind=kOutput, calls=%fused_computation.2 | convolution fusion | flops 6445596672 | bytes 13631488 | tf_op jit(solution)/shard_map/dot_general | solution.py:1069
  392.1 8.5 %convolution_convert_fusion.1 = bf16[1024,2048]{1,0:T(8,128)(2,1)} fusion(bf16[1024,1536]{1,0:T(8,128)(2,1)S(1)} %constant_dynamic-update-slice_fusion, bf16[2048,1536]{1,0:T(8,128)(2,1)S(1)} %bitcast.190), kind=kOutput, calls=%fused_computation.3 | convolution fusion | flops 6444548096 | bytes 13631488 | tf_op jit(solution)/shard_map/dot_general | solution.py:1065
  400.6 1.0 collective-permute-start.4
  401.7 4.3 convolution_convert_fusion.2
  406.4 1.1 pad_maximum_fusion.1.out_q
  407.4 17.7 %collective-permute-done.4 = bf16[8,64,512]{2,1,0:T(8,128)(2,1)S(1)} collective-permute-done((bf16[8,64,512]{2,1,0:T(8,128)(2,1)S(1)}, bf16[8,64,512]{2,1,0:T(8,128)(2,1)S(1)}, u32[]{:S(2)}, u32[]{:S(2)}) %collective-permute-start.4) | collective-permute-done | bytes 524320 | tf_op jit(solution)/shard_map/ppermute | solution.py:1145
  425.2 1.0 add_convert_fusion.2.up_sum
  426.1 130.6 %closing.1 = (bf16[64,2048]{1,0:T(8,128)(2,1)}, bf16[64,2048]{1,0:T(8,128)(2,1)}, bf16[64,4096]{1,0:T(8,128)(2,1)}, bf16[64,4096]{1,0:T(8,128)(2,1)}, bf16[8,64,...) custom-call(bf16[4,8,64,1536]{3,2,1,0:T(8,128)(2,1)} %bitcast.150, ...), custom_call_target="tpu_custom_call" | custom-call | tf_op jit(solution)/shard_map/closing/pallas_call | solution.py:1008
  556.8 2.1 convert_element_type.215
  558.9 1.9 collective-permute-start.5
  560.8 0.8 constant_dynamic-slice_fusion
  562.1 1.7 reshape.846
  563.7 0.7 copy.93
  564.4 1.4 reshape.840
  566.5 0.7 copy.94
  567.2 1.4 reshape.842
  568.7 0.9 copy-done.23
  569.6 1.0 convert_element_type.213
  570.7 1.0 convert_element_type.214
  571.7 0.8 convert_element_type.211
  572.5 0.8 convert_element_type.212
  573.4 0.9 fusion.18
  574.3 11.7 %collective-permute-done.5 = bf16[128,2048]{1,0:T(8,128)(2,1)} collective-permute-done((bf16[128,2048]{1,0:T(8,128)(2,1)}, bf16[128,2048]{1,0:T(8,128)(2,1)}, u32[]{:S(2)}, u32[]{:S(2)}) %collective-permute-start.5) | collective-permute-done | bytes 524320 | tf_op jit(solution)/shard_map/ppermute | solution.py:1289
  586.0 2.1 convert_element_type.217
  588.1 1.0 copy.111
  589.1 1.0 copy.112
  (158 shorter events, 14.3 us)
Async XLA Ops:
  0.6 11.0 %copy-start.25 = (bf16[64,4096]{1,0:T(8,128)(2,1)S(1)}, bf16[64,4096]{1,0:T(8,128)(2,1)}, u32[]{:S(2)}) copy-start(bf16[64,4096]{1,0:T(8,128)(2,1)} %param.27) | copy-start | bytes 1572868
  0.7 15.1 %collective-permute-start = (bf16[128,2048]{1,0:T(8,128)(2,1)}, bf16[128,2048]{1,0:T(8,128)(2,1)S(1)}, u32[]{:S(2)}, u32[]{:S(2)}) collective-permute-start(bf16[128,2048]{1,0:T(8,128)(2,1)} %param.23), channel_id=1, source_target_pairs={{0,0},{1,16},{2,4},{3,20},{4,1},{5,17},{6,5},{7,21},{8,2},{9,18},{... | collective-permute-start | bytes 1572872 | tf_op jit(solution)/shard_map/ppermute | solution.py:1132
  10.7 4.1 copy-start.26
  15.8 0.8 copy-start.27
  141.4 28.0 %collective-permute-start.1 = (bf16[128,2048]{1,0:T(8,128)(2,1)}, bf16[128,2048]{1,0:T(8,128)(2,1)}, u32[]{:S(2)}, u32[]{:S(2)}) collective-permute-start(bf16[128,2048]{1,0:T(8,128)(2,1)} %param.28), channel_id=1, source_target_pairs={{0,16},{1,17},{2,18},{3,19},{4,20},{5,21},{6,22},{7,23},{8,24},{9,... | collective-permute-start | bytes 1572872 | tf_op jit(solution)/shard_map/ppermute | solution.py:1145
  144.9 10.6 %copy-start.1 = (f32[1024,128]{1,0:T(8,128)}, f32[1024,128]{1,0:T(8,128)S(1)}, u32[]{:S(2)}) copy-start(f32[1024,128]{1,0:T(8,128)S(1)} %get-tuple-element.54) | copy-start | bytes 1572868
  144.9 10.6 %copy-start.3 = (f32[1024,128]{1,0:T(8,128)}, f32[1024,128]{1,0:T(8,128)S(1)}, u32[]{:S(2)}) copy-start(f32[1024,128]{1,0:T(8,128)S(1)} %get-tuple-element.53) | copy-start | bytes 1572868
  155.3 2.6 copy-start
  155.5 4.2 copy-start.6
  158.0 1.7 copy-start.11
  158.0 1.7 copy-start.13
  158.0 1.7 copy-start.15
  159.7 0.7 copy-start.20
  161.0 4.0 copy-start.34
  163.6 5.7 copy-start.8
  246.7 5.3 copy-start.33
  246.8 5.3 copy-start.37
  252.1 2.3 copy-start.31
  252.1 2.9 copy-start.35
  255.0 3.8 copy-start.38
  258.8 8.8 %copy-start.40 = (bf16[1024,512]{1,0:T(8,128)(2,1)}, bf16[1024,512]{1,0:T(8,128)(2,1)S(1)}, u32[]{:S(2)}) copy-start(bf16[1024,512]{1,0:T(8,128)(2,1)S(1)} %get-tuple-element.93) | copy-start | bytes 3145732
  370.2 1.0 copy-start.21
  370.2 1.4 copy-start.7
  371.6 1.8 copy-start.14
  371.6 1.8 copy-start.16
  371.6 2.1 copy-start.12
  371.7 2.4 copy-start.32
  373.4 1.4 copy-start.9
  374.8 2.4 copy-start.4
  377.4 1.0 copy-start.2
  379.1 26.9 %collective-permute-start.2 = (bf16[4,32,2048]{2,1,0:T(8,128)(2,1)S(1)}, bf16[4,32,2048]{2,1,0:T(8,128)(2,1)S(1)}, u32[]{:S(2)}, u32[]{:S(2)}) collective-permute-start(bf16[4,32,2048]{2,1,0:T(8,128)(2,1)S(1)} %get-tuple-element.98), channel_id=1, source_target_pairs={{0,4},{1,5},{2,6},{3,7},{4,0},{5,1},{6,2},{7,3},{8,12},{9,13},{10,... | collective-permute-start | bytes 1572872 | tf_op jit(solution)/shard_map/ppermute | solution.py:1145
  379.2 26.7 %collective-permute-start.3 = (bf16[4,32,2048]{2,1,0:T(8,128)(2,1)S(1)}, bf16[4,32,2048]{2,1,0:T(8,128)(2,1)S(1)}, u32[]{:S(2)}, u32[]{:S(2)}) collective-permute-start(bf16[4,32,2048]{2,1,0:T(8,128)(2,1)S(1)} %get-tuple-element.99), channel_id=1, source_target_pairs={{0,4},{1,5},{2,6},{3,7},{4,0},{5,1},{6,2},{7,3},{8,12},{9,13},{10,... | collective-permute-start | bytes 1572872 | tf_op jit(solution)/shard_map/ppermute | solution.py:1145
  381.2 2.2 copy-start.30
  381.2 10.9 %slice-start = ((s8[6291456]{0:T(1024)(128)(4,1)}), s8[4194304]{0:T(1024)(128)(4,1)S(1)}, s32[]{:S(2)}) async-start(s8[6291456]{0:T(1024)(128)(4,1)} %bitcast.188), calls=%async_computation | async-start | bytes 8388608
  383.4 8.7 %slice-start.1 = ((s8[6291456]{0:T(1024)(128)(4,1)}), s8[2097152]{0:T(1024)(128)(4,1)S(1)}, s32[]{:S(2)}) async-start(s8[6291456]{0:T(1024)(128)(4,1)} %bitcast.188), calls=%async_computation.1 | async-start | bytes 4194304
  392.0 8.6 %copy-start.39 = (bf16[1,8,64,512]{3,2,1,0:T(8,128)(2,1)S(1)}, bf16[1,8,64,512]{3,2,1,0:T(8,128)(2,1)}, u32[]{:S(2)}) copy-start(bf16[1,8,64,512]{3,2,1,0:T(8,128)(2,1)} %get-tuple-element.68) | copy-start | bytes 1572868
  392.1 9.6 %copy-start.36 = (bf16[4,128,2048]{2,1,0:T(8,128)(2,1)S(1)}, bf16[4,128,2048]{2,1,0:T(8,128)(2,1)}, u32[]{:S(2)}) copy-start(bf16[4,128,2048]{2,1,0:T(8,128)(2,1)} %get-tuple-element.61) | copy-start | bytes 6291460
  392.1 9.6 %copy-start.41 = (bf16[1024,512]{1,0:T(8,128)(2,1)S(1)}, bf16[1024,512]{1,0:T(8,128)(2,1)}, u32[]{:S(2)}) copy-start(bf16[1024,512]{1,0:T(8,128)(2,1)} %copy-done.40) | copy-start | bytes 3145732
  400.6 24.5 %collective-permute-start.4 = (bf16[8,64,512]{2,1,0:T(8,128)(2,1)S(1)}, bf16[8,64,512]{2,1,0:T(8,128)(2,1)S(1)}, u32[]{:S(2)}, u32[]{:S(2)}) collective-permute-start(bf16[8,64,512]{2,1,0:T(8,128)(2,1)S(1)} %bitcast.208), channel_id=1, source_target_pairs={{0,16},{1,17},{2,18},{3,19},{4,20},{5,21},{6,22},{7,23},{8,24},{9,... | collective-permute-start | bytes 1572872 | tf_op jit(solution)/shard_map/ppermute | solution.py:1145
  406.0 19.2 %copy-start.18 = (f32[8,64,512]{2,1,0:T(8,128)S(1)}, f32[8,64,512]{2,1,0:T(8,128)}, u32[]{:S(2)}) copy-start(f32[8,64,512]{2,1,0:T(8,128)} %get-tuple-element.67) | copy-start | bytes 3145732
  558.9 27.1 %collective-permute-start.5 = (bf16[128,2048]{1,0:T(8,128)(2,1)}, bf16[128,2048]{1,0:T(8,128)(2,1)}, u32[]{:S(2)}, u32[]{:S(2)}) collective-permute-start(bf16[128,2048]{1,0:T(8,128)(2,1)} %bitcast.70), channel_id=1, source_target_pairs={{0,0},{16,1},{4,2},{20,3},{1,4},{17,5},{5,6},{21,7},{2,8},{18,9},{... | collective-permute-start | bytes 1572872 | tf_op jit(solution)/shard_map/ppermute | solution.py:1289
  563.7 2.1 copy-start.24
  566.5 2.1 copy-start.5
  567.2 1.4 copy-start.10
  568.6 1.0 copy-start.23
  568.6 2.1 copy-start.22
  568.7 3.0 copy-start.29
  568.7 3.8 copy-start.28
  572.5 15.5 %copy-start.19 = (f32[2,64,2048]{2,1,0:T(8,128)S(1)}, f32[2,64,2048]{2,1,0:T(8,128)}, u32[]{:S(2)}) copy-start(f32[2,64,2048]{2,1,0:T(8,128)} %get-tuple-element.72) | copy-start | bytes 3145732
  574.3 14.8 %copy-start.17 = (f32[4,32,2048]{2,1,0:T(8,128)S(1)}, f32[4,32,2048]{2,1,0:T(8,128)}, u32[]{:S(2)}) copy-start(f32[4,32,2048]{2,1,0:T(8,128)} %get-tuple-element.81) | copy-start | bytes 3145732
